TPU v7x, 16 devices: a whole 2x2x2 slice. The times are simulated.
16 devices in a mesh: dp: 16 (over z, y, x, core).
Axes of the slice: x: 2, y: 2, z: 2, core: 2. Of those that a mesh axis runs over, the one named last changes fastest.
Arguments:
- grad_embed: bfloat16 [16, 16384, 640], P('dp')
- grad_q: bfloat16 [16, 6, 640, 64], P('dp')
- grad_k: bfloat16 [16, 6, 640, 16], P('dp')
- grad_v: bfloat16 [16, 6, 640, 16], P('dp')
- grad_out: bfloat16 [16, 6, 64, 640], P('dp')
- grad_gate: bfloat16 [16, 6, 640, 128], P('dp')
- grad_up: bfloat16 [16, 6, 640, 128], P('dp')
- grad_down: bfloat16 [16, 6, 128, 640], P('dp')
- grad_norms: bfloat16 [16, 6, 4, 640], P('dp')
- grad_qk_norms: bfloat16 [16, 6, 2, 256], P('dp')
- first_moment: float32 [12593152], P('dp')
- second_moment: float32 [12593152], P('dp')
- master_param: float32 [12593152], P('dp')
- hyper_params: float32 [5], replicated
Outputs:
- output 1: bfloat16 [16384, 640], replicated
- output 2: bfloat16 [6, 640, 64], replicated
- output 3: bfloat16 [6, 640, 16], replicated
- output 4: bfloat16 [6, 640, 16], replicated
- output 5: bfloat16 [6, 64, 640], replicated
- output 6: bfloat16 [6, 640, 128], replicated
- output 7: bfloat16 [6, 640, 128], replicated
- output 8: bfloat16 [6, 128, 640], replicated
- output 9: bfloat16 [6, 4, 640], replicated
- output 10: bfloat16 [6, 2, 256], replicated
- output 11: float32 [12593152], P('dp')
- output 12: float32 [12593152], P('dp')
- output 13: float32 [12593152], P('dp')
All inputs are finite; a program needn't handle non-finite values.
Results may differ from a plain program's by a relative error of at most 0.001.
Values are sent between devices in bfloat16 or wider.
A program may use at most 1 GiB of HBM per device.

v0:
```python
import math
import jax
import jax.numpy as jnp
from jax import lax
from jax.sharding import PartitionSpec as P

ADAM_STEP = 7
ADAM_EPS = 1e-8
CLIP_EPS = 1e-6
GRAD_COUNT = 10
NORM_COUNT = 2


def adam_step(grad_part, first_part, second_part, master_part, hyper_params, clip_scale, keep_decay):
    learn_rate = hyper_params[0]
    beta_one = hyper_params[1]
    beta_two = hyper_params[2]
    weight_decay = hyper_params[3]
    clipped = grad_part * clip_scale
    moment_one = beta_one * first_part + (1.0 - beta_one) * clipped
    moment_two = beta_two * second_part + (1.0 - beta_two) * (clipped * clipped)
    m_hat = moment_one / (1.0 - beta_one ** ADAM_STEP)
    v_hat = moment_two / (1.0 - beta_two ** ADAM_STEP)
    direction = m_hat / (jnp.sqrt(v_hat) + ADAM_EPS) + jnp.where(keep_decay, weight_decay * master_part, 0.0)
    new_master = master_part - learn_rate * direction
    return moment_one, moment_two, new_master


def split_params(joined, shapes):
    pieces = []
    start_pos = 0
    for tensor_dims in shapes:
        tensor_size = math.prod(tensor_dims)
        pieces.append(joined[start_pos:start_pos + tensor_size].reshape(tensor_dims))
        start_pos = start_pos + tensor_size
    return pieces


def solution(mesh):
    group_size = mesh.shape["dp"]

    def local_update(*arrays):
        grads = arrays[:GRAD_COUNT]
        first_part, second_part, master_part, hyper_params = arrays[GRAD_COUNT:]
        shapes = [grad_arr.shape[1:] for grad_arr in grads]
        sizes = [math.prod(tensor_dims) for tensor_dims in shapes]
        total_len = sum(sizes)
        shard_len = total_len // group_size
        decay_len = total_len - sum(sizes[GRAD_COUNT - NORM_COUNT:])
        local_vec = jnp.concatenate([grad_arr.reshape(-1) for grad_arr in grads]).reshape(group_size, shard_len)
        received = lax.all_to_all(local_vec, "dp", 0, 0, tiled=True)
        grad_part = jnp.sum(received, axis=0, dtype=jnp.float32) / group_size
        square_sum = lax.psum(jnp.sum(grad_part * grad_part), "dp")
        clip_scale = jnp.minimum(1.0, hyper_params[4] / (jnp.sqrt(square_sum) + CLIP_EPS))
        offset = lax.axis_index("dp") * shard_len
        keep_decay = offset + lax.broadcasted_iota(jnp.int32, (shard_len,), 0) < decay_len
        moment_one, moment_two, new_master = adam_step(grad_part, first_part, second_part, master_part, hyper_params, clip_scale, keep_decay)
        full_vec = lax.all_gather(new_master.astype(jnp.bfloat16), "dp", tiled=True)
        return tuple(split_params(full_vec, shapes)) + (moment_one, moment_two, new_master)

    in_specs = tuple([P("dp")] * GRAD_COUNT + [P("dp"), P("dp"), P("dp"), P()])
    out_specs = tuple([P()] * GRAD_COUNT + [P("dp"), P("dp"), P("dp")])
    return jax.shard_map(local_update, mesh=mesh, in_specs=in_specs, out_specs=out_specs, check_vma=False)
```

profile of v0, /device:TPU:0, one launch (start us, length us, event | category | flops | bytes accessed | tf_op | source)
XLA Modules:
  0.0 1828.6 jit_solution(8287231209777075789)
XLA Ops:
  7.2 34.3 %reshape.97 = bf16[10485760]{0:T(1024)(128)(2,1)} reshape(bf16[1,16384,640]{2,1,0:T(8,128)(2,1)} %param.14) | data formatting | bytes 41943040 | tf_op jit(solution)/shard_map/reshape | solution.py:50
  41.5 17.2 constant_dynamic-update-slice_fusion.9
  72.5 336.8 %while.1 = (u32[]{:T(128)}, bf16[12593152]{0:T(1024)(128)(2,1)}, bf16[16,1,787072]{2,1,0:T(2,128)(2,1)}, u32[]{}, u32[]{}) while((u32[]{:T(128)}, bf16[12593152]{0:T(1024)(128)(2,1)}, bf16[16,1,787072]{2,1,0:T(2,128)(2,1)}, u32[]{}, u32[]{}) %tuple.32), condition=%wide.cond, body=%wide.body.sunk | while | flops 9 | bytes 7870885
  74.8 18.8 %reshape_dynamic-update-slice_fusion.2 = bf16[16,1,787072]{2,1,0:T(2,128)(2,1)} fusion(bf16[16,1,787072]{2,1,0:T(2,128)(2,1)} %get-tuple-element.92, u32[]{:T(128)S(6)} %multiply.17, u32[]{:T(128)S(6)} %multiply.18, bf16[787072]{0:T(1024)(128)(2,1)S(1)} %dynamic-slice.2), kind=kLoop, calls=%fused_computation.21.clone.1 | loop fusion | bytes 4722440
  95.9 18.8 %reshape_dynamic-update-slice_fusion.2 = bf16[16,1,787072]{2,1,0:T(2,128)(2,1)} fusion(bf16[16,1,787072]{2,1,0:T(2,128)(2,1)} %get-tuple-element.92, u32[]{:T(128)S(6)} %multiply.17, u32[]{:T(128)S(6)} %multiply.18, bf16[787072]{0:T(1024)(128)(2,1)S(1)} %dynamic-slice.2), kind=kLoop, calls=%fused_computation.21.clone.1 | loop fusion | bytes 4722440
  116.9 18.8 %reshape_dynamic-update-slice_fusion.2 = bf16[16,1,787072]{2,1,0:T(2,128)(2,1)} fusion(bf16[16,1,787072]{2,1,0:T(2,128)(2,1)} %get-tuple-element.92, u32[]{:T(128)S(6)} %multiply.17, u32[]{:T(128)S(6)} %multiply.18, bf16[787072]{0:T(1024)(128)(2,1)S(1)} %dynamic-slice.2), kind=kLoop, calls=%fused_computation.21.clone.1 | loop fusion | bytes 4722440
  138.0 18.8 %reshape_dynamic-update-slice_fusion.2 = bf16[16,1,787072]{2,1,0:T(2,128)(2,1)} fusion(bf16[16,1,787072]{2,1,0:T(2,128)(2,1)} %get-tuple-element.92, u32[]{:T(128)S(6)} %multiply.17, u32[]{:T(128)S(6)} %multiply.18, bf16[787072]{0:T(1024)(128)(2,1)S(1)} %dynamic-slice.2), kind=kLoop, calls=%fused_computation.21.clone.1 | loop fusion | bytes 4722440
  159.0 18.8 %reshape_dynamic-update-slice_fusion.2 = bf16[16,1,787072]{2,1,0:T(2,128)(2,1)} fusion(bf16[16,1,787072]{2,1,0:T(2,128)(2,1)} %get-tuple-element.92, u32[]{:T(128)S(6)} %multiply.17, u32[]{:T(128)S(6)} %multiply.18, bf16[787072]{0:T(1024)(128)(2,1)S(1)} %dynamic-slice.2), kind=kLoop, calls=%fused_computation.21.clone.1 | loop fusion | bytes 4722440
  180.1 18.8 %reshape_dynamic-update-slice_fusion.2 = bf16[16,1,787072]{2,1,0:T(2,128)(2,1)} fusion(bf16[16,1,787072]{2,1,0:T(2,128)(2,1)} %get-tuple-element.92, u32[]{:T(128)S(6)} %multiply.17, u32[]{:T(128)S(6)} %multiply.18, bf16[787072]{0:T(1024)(128)(2,1)S(1)} %dynamic-slice.2), kind=kLoop, calls=%fused_computation.21.clone.1 | loop fusion | bytes 4722440
  201.1 18.8 %reshape_dynamic-update-slice_fusion.2 = bf16[16,1,787072]{2,1,0:T(2,128)(2,1)} fusion(bf16[16,1,787072]{2,1,0:T(2,128)(2,1)} %get-tuple-element.92, u32[]{:T(128)S(6)} %multiply.17, u32[]{:T(128)S(6)} %multiply.18, bf16[787072]{0:T(1024)(128)(2,1)S(1)} %dynamic-slice.2), kind=kLoop, calls=%fused_computation.21.clone.1 | loop fusion | bytes 4722440
  222.2 18.8 %reshape_dynamic-update-slice_fusion.2 = bf16[16,1,787072]{2,1,0:T(2,128)(2,1)} fusion(bf16[16,1,787072]{2,1,0:T(2,128)(2,1)} %get-tuple-element.92, u32[]{:T(128)S(6)} %multiply.17, u32[]{:T(128)S(6)} %multiply.18, bf16[787072]{0:T(1024)(128)(2,1)S(1)} %dynamic-slice.2), kind=kLoop, calls=%fused_computation.21.clone.1 | loop fusion | bytes 4722440
  243.3 18.8 %reshape_dynamic-update-slice_fusion.2 = bf16[16,1,787072]{2,1,0:T(2,128)(2,1)} fusion(bf16[16,1,787072]{2,1,0:T(2,128)(2,1)} %get-tuple-element.92, u32[]{:T(128)S(6)} %multiply.17, u32[]{:T(128)S(6)} %multiply.18, bf16[787072]{0:T(1024)(128)(2,1)S(1)} %dynamic-slice.2), kind=kLoop, calls=%fused_computation.21.clone.1 | loop fusion | bytes 4722440
  264.3 18.8 %reshape_dynamic-update-slice_fusion.2 = bf16[16,1,787072]{2,1,0:T(2,128)(2,1)} fusion(bf16[16,1,787072]{2,1,0:T(2,128)(2,1)} %get-tuple-element.92, u32[]{:T(128)S(6)} %multiply.17, u32[]{:T(128)S(6)} %multiply.18, bf16[787072]{0:T(1024)(128)(2,1)S(1)} %dynamic-slice.2), kind=kLoop, calls=%fused_computation.21.clone.1 | loop fusion | bytes 4722440
  285.3 18.8 %reshape_dynamic-update-slice_fusion.2 = bf16[16,1,787072]{2,1,0:T(2,128)(2,1)} fusion(bf16[16,1,787072]{2,1,0:T(2,128)(2,1)} %get-tuple-element.92, u32[]{:T(128)S(6)} %multiply.17, u32[]{:T(128)S(6)} %multiply.18, bf16[787072]{0:T(1024)(128)(2,1)S(1)} %dynamic-slice.2), kind=kLoop, calls=%fused_computation.21.clone.1 | loop fusion | bytes 4722440
  306.4 18.8 %reshape_dynamic-update-slice_fusion.2 = bf16[16,1,787072]{2,1,0:T(2,128)(2,1)} fusion(bf16[16,1,787072]{2,1,0:T(2,128)(2,1)} %get-tuple-element.92, u32[]{:T(128)S(6)} %multiply.17, u32[]{:T(128)S(6)} %multiply.18, bf16[787072]{0:T(1024)(128)(2,1)S(1)} %dynamic-slice.2), kind=kLoop, calls=%fused_computation.21.clone.1 | loop fusion | bytes 4722440
  327.4 18.8 %reshape_dynamic-update-slice_fusion.2 = bf16[16,1,787072]{2,1,0:T(2,128)(2,1)} fusion(bf16[16,1,787072]{2,1,0:T(2,128)(2,1)} %get-tuple-element.92, u32[]{:T(128)S(6)} %multiply.17, u32[]{:T(128)S(6)} %multiply.18, bf16[787072]{0:T(1024)(128)(2,1)S(1)} %dynamic-slice.2), kind=kLoop, calls=%fused_computation.21.clone.1 | loop fusion | bytes 4722440
  348.5 18.8 %reshape_dynamic-update-slice_fusion.2 = bf16[16,1,787072]{2,1,0:T(2,128)(2,1)} fusion(bf16[16,1,787072]{2,1,0:T(2,128)(2,1)} %get-tuple-element.92, u32[]{:T(128)S(6)} %multiply.17, u32[]{:T(128)S(6)} %multiply.18, bf16[787072]{0:T(1024)(128)(2,1)S(1)} %dynamic-slice.2), kind=kLoop, calls=%fused_computation.21.clone.1 | loop fusion | bytes 4722440
  369.6 18.8 %reshape_dynamic-update-slice_fusion.2 = bf16[16,1,787072]{2,1,0:T(2,128)(2,1)} fusion(bf16[16,1,787072]{2,1,0:T(2,128)(2,1)} %get-tuple-element.92, u32[]{:T(128)S(6)} %multiply.17, u32[]{:T(128)S(6)} %multiply.18, bf16[787072]{0:T(1024)(128)(2,1)S(1)} %dynamic-slice.2), kind=kLoop, calls=%fused_computation.21.clone.1 | loop fusion | bytes 4722440
  390.6 18.8 %reshape_dynamic-update-slice_fusion.2 = bf16[16,1,787072]{2,1,0:T(2,128)(2,1)} fusion(bf16[16,1,787072]{2,1,0:T(2,128)(2,1)} %get-tuple-element.92, u32[]{:T(128)S(6)} %multiply.17, u32[]{:T(128)S(6)} %multiply.18, bf16[787072]{0:T(1024)(128)(2,1)S(1)} %dynamic-slice.2), kind=kLoop, calls=%fused_computation.21.clone.1 | loop fusion | bytes 4722440
  409.9 151.7 %reduce.2 = bf16[16,787072]{1,0:T(8,128)(2,1)} reduce(bf16[16,1,787072]{2,1,0:T(2,128)(2,1)} %get-tuple-element.43, bf16[]{:T(256)} %broadcast.3), dimensions={1}, to_apply=%get-tuple-element.43.reduce_sub_computation | reduce | bytes 50372608 | tf_op jit(solution)/shard_map/all_to_all | solution.py:51
  561.6 73.1 %reshape.120 = bf16[16,2,393536]{2,1,0:T(2,128)(2,1)} reshape(bf16[16,787072]{1,0:T(8,128)(2,1)} %reduce.2) | data formatting | bytes 50372608
  645.9 298.4 %all-to-all-done = bf16[16,2,393536]{2,1,0:T(2,128)(2,1)} async-done(((bf16[16,2,393536]{2,1,0:T(2,128)(2,1)}), bf16[16,2,393536]{2,1,0:T(2,128)(2,1)}, u32[]{:S(2)}, u32[]{:S(2)}) %all-to-all-start) | async-done | bytes 25186336 | tf_op jit(solution)/shard_map/all_to_all | solution.py:51
  944.3 88.0 %reshape.121 = bf16[16,1,787072]{2,1,0:T(2,128)(2,1)} reshape(bf16[16,2,393536]{2,1,0:T(2,128)(2,1)} %all-to-all-done) | data formatting | bytes 50372608
  1032.3 260.9 %convert_reduce_fusion = f32[787072]{0:T(1024)S(1)} fusion(bf16[16,1,787072]{2,1,0:T(2,128)(2,1)} %reshape.121), kind=kLoop, calls=%fused_computation | loop fusion | flops 24399232 | bytes 28334592 | tf_op jit(solution)/shard_map/reduce_sum | solution.py:52
  1294.6 35.2 %psum.7 = f32[]{:T(128)} all-reduce(f32[]{:T(128)} %multiply_reduce_fusion), channel_id=1, replica_groups=mesh['dp'=16] {'dp'}, use_global_device_ids=true, to_apply=%region_2.0 | all-reduce | flops 1 | bytes 8 | tf_op jit(solution)/shard_map/psum | solution.py:53
  1331.1 10.1 fusion
  1341.2 18.7 %reshape.116 = bf16[1,1,787072]{2,1,0:T(2,128)(2,1)} reshape(bf16[787072]{0:T(1024)(128)(2,1)S(1)} %get-tuple-element.50) | data formatting | bytes 3148288
  1359.9 187.8 %all-gather.3.cloned.1.call-done = bf16[16,1,787072]{2,1,0:T(2,128)(2,1)} async-done(((bf16[1,1,787072]{2,1,0:T(2,128)(2,1)}), bf16[16,1,787072]{2,1,0:T(2,128)(2,1)}) %all-gather.3.cloned.1.call-update) | async-done | bytes 25186320 | tf_op jit(solution)/shard_map/all_gather | solution.py:58
  1547.7 151.1 %reduce.1 = bf16[16,787072]{1,0:T(8,128)(2,1)} reduce(bf16[16,1,787072]{2,1,0:T(2,128)(2,1)} %all-gather.3.cloned.1.call-done, bf16[]{:T(256)} %constant.29), dimensions={1}, to_apply=%all-gather.reduce_sub_computation | reduce | bytes 50372608 | tf_op jit(solution)/shard_map/all_gather | solution.py:58
  1698.8 55.8 %reshape.117 = bf16[12593152]{0:T(1024)(128)(2,1)} reshape(bf16[16,787072]{1,0:T(8,128)(2,1)} %reduce.1) | data formatting | bytes 50372608
  1754.6 18.2 slice.71
  1778.2 34.3 %reshape.107 = bf16[16384,640]{1,0:T(8,128)(2,1)} reshape(bf16[10485760]{0:T(1024)(128)(2,1)} %slice.71) | data formatting | bytes 41943040 | tf_op jit(solution)/shard_map/reshape | solution.py:34
  (83 shorter events, 72.1 us)
Async XLA Ops:
  41.5 17.2 copy-start.4
  41.5 18.1 copy-start.7
  58.7 2.7 copy-start.8
  59.1 4.1 copy-start.5
  59.1 4.4 copy-start.1
  60.1 4.2 copy-start.9
  60.1 4.2 copy-start.11
  63.6 3.2 copy-start.6
  64.3 3.9 copy-start.2
  64.3 4.9 copy-start.3
  634.7 5.4 copy-start.10
  634.7 309.5 %all-to-all-start = ((bf16[16,2,393536]{2,1,0:T(2,128)(2,1)}), bf16[16,2,393536]{2,1,0:T(2,128)(2,1)}, u32[]{:S(2)}, u32[]{:S(2)}) async-start(bf16[16,2,393536]{2,1,0:T(2,128)(2,1)} %reshape.120), calls=%async_computation | async-start | bytes 50380800 | tf_op jit(solution)/shard_map/all_to_all | solution.py:51
  640.1 907.6 %all-gather.3.cloned.1.call-start = ((), (), s32[]{:S(2)}) async-start(), calls=%async_computation.1 | async-start | bytes 53520896 | tf_op jit(solution)/shard_map/all_gather | solution.py:58
  1754.6 22.0 %copy-start = (bf16[12593152]{0:T(1024)(128)(2,1)S(1)}, bf16[12593152]{0:T(1024)(128)(2,1)}, u32[]{:S(2)}) copy-start(bf16[12593152]{0:T(1024)(128)(2,1)} %reshape.117) | copy-start | bytes 75558912
  1814.7 5.4 slice-start
  1814.7 6.0 slice-start.1
Sparse Core Ops, SparseCore 0:
  1360.0 187.5 all-gather.2
where the time goes:
time: 1840 us; the launch traced here: 1830 us
  local copies, waits for them, and re-layouts  705 us (38%)
  other arithmetic  575 us (31%)
  waiting for transfers between devices  486 us (26%)
  blocking collectives  35.2 us (2%)
  between operations  21.3 us (1%)
    unnamed x76, local copies, waits for them, and re-layouts  606 us
    all_to_all x1, waiting for transfers between devices, local_update(): received = lax.all_to_all(local_vec, 'dp', 0, 0, tiled=True)  298 us
    reduce_sum x1, other arithmetic, local_update(): grad_part = jnp.sum(received, axis=0, dtype=jnp.float32) / group_size  261 us
    all_gather x1, waiting for transfers between devices, local_update(): full_vec = lax.all_gather(new_master.astype(jnp.bfloat16), 'dp', tiled=True)  188 us
    all_to_all x1, other arithmetic, local_update(): received = lax.all_to_all(local_vec, 'dp', 0, 0, tiled=True)  152 us
    all_gather x1, other arithmetic, local_update(): full_vec = lax.all_gather(new_master.astype(jnp.bfloat16), 'dp', tiled=True)  151 us
    reshape x7, local copies, waits for them, and re-layouts, split_params(): joined[start_pos:start_pos + tensor_size].reshape(tensor_dims)  39.4 us
    reshape x7, local copies, waits for them, and re-layouts, local_update(): grad_arr.reshape(-1)  38.4 us
  transfers between devices with their start and end apart: 2, of which 2 were waited for; matrix products, arithmetic and copies ran while one was open for 0% of the time, Pallas kernels for 0%

commit v1 on v0

v1 whole, which is shorter than its diff:
```python
import functools
import math
import jax
import jax.numpy as jnp
from jax import lax
from jax.experimental import pallas as pl
from jax.experimental.pallas import tpu as pltpu
from jax.sharding import PartitionSpec as P

ADAM_STEP = 7
ADAM_EPS = 1e-8
CLIP_EPS = 1e-6
GRAD_COUNT = 10
MESH = pl.DeviceIdType.MESH

DEVS = 16
WIDTH = 640
SHARD_ROWS = 6149
TILE_ROWS = 40
EMBED_TILES = 2048
ALL_TILES = 2460
DECAY_ROWS = 98240
FIRST_TAIL = 13
TAIL_START = (SHARD_ROWS * FIRST_TAIL) // TILE_ROWS
RS_TILES = 52
TAIL_TILES = (SHARD_ROWS * 15) // TILE_ROWS + 3 * RS_TILES - TAIL_START
AG_TILES = 51
LEAD = 40
G_ROWS = LEAD + 3 * RS_TILES * TILE_ROWS
ORDERS = ((2, 4, 8), (4, 8, 2), (8, 2, 4))


def flip(dev, stride):
    return dev + stride - 2 * stride * lax.rem(dev // stride, 2)


def rs_start(dev):
    return (SHARD_ROWS * dev) // TILE_ROWS


def ag_start(dev):
    return (SHARD_ROWS * dev + TILE_ROWS - 1) // TILE_ROWS


def flip_mask(dev, order, mask):
    for bit, stride in enumerate(order):
        if mask >> bit & 1:
            dev = flip(dev, stride)
    return dev


def kernel(emb, tail, m_in, v_in, p_in, hyp, vout, m_out, v_out, p_out,
           own, r1, s1, r2, r3, mom, vel, par, ext, grad, stage, nsend, nrecv,
           own_sem, r1_send, r1_recv, r2_send, r2_recv, r3_send, r3_recv, st_sem,
           ext_send, ext_recv, n_send, n_recv, ag_send, ag_recv, d2d_send, d2d_recv, loc_sem):
    me = lax.axis_index("dp")
    partner = flip(me, 1)

    def remote(src, dst, ssem, rsem, dev):
        return pltpu.make_async_remote_copy(
            src_ref=src, dst_ref=dst, send_sem=ssem, recv_sem=rsem, device_id=(dev,), device_id_type=MESH)

    def from_shard(owner, k, make):
        first = rs_start(owner) + k * RS_TILES

        @pl.when(owner < FIRST_TAIL)
        def _():
            make(emb.at[pl.ds(first, RS_TILES)]).start()

        @pl.when(owner >= FIRST_TAIL)
        def _():
            make(tail.at[pl.ds(first - TAIL_START, RS_TILES)]).start()

    def rs_owner(dev, k, f):
        return flip_mask(dev, ORDERS[k], (0 if f >= 2 else 2) + (4 if f % 2 == 0 else 0))

    state = [pltpu.make_async_copy(src, dst, st_sem.at[i])
             for i, (src, dst) in enumerate(((m_in, mom), (v_in, vel), (p_in, par)))]

    for f in range(4):
        for k in range(3):
            from_shard(rs_owner(me, k, f), k,
                       lambda src, k=k, f=f: pltpu.make_async_copy(src, own.at[k, f], own_sem.at[k, f]))
    barrier = pltpu.get_barrier_semaphore()
    for j in range(1, DEVS):
        pl.semaphore_signal(barrier, inc=1, device_id=(lax.rem(me + j, DEVS),), device_id_type=MESH)
    pl.semaphore_wait(barrier, DEVS - 1)

    for f in range(4):
        for k in range(3):
            for slot in range(3):
                dev = partner if slot == 2 else flip(me, ORDERS[k][0])
                if slot == 1:
                    dev = flip(dev, 1)
                from_shard(rs_owner(dev, k, f), k, lambda src, k=k, f=f, slot=slot, dev=dev: remote(
                    src, r1.at[slot, k, f], r1_send.at[slot, k, f], r1_recv.at[slot, k, f], dev))
    before = lax.rem(me + DEVS - 1, DEVS)
    ext_copies = [remote(src.at[pl.ds(0, TILE_ROWS)], ext.at[i], ext_send.at[i], ext_recv.at[i], before)
                  for i, src in enumerate((m_in, v_in, p_in))]
    for copy in ext_copies:
        copy.start()
    for copy in state:
        copy.start()

    def r1_copy(slot, k, f):
        return remote(emb.at[pl.ds(0, RS_TILES)], r1.at[slot, k, f], r1_send.at[slot, k, f],
                      r1_recv.at[slot, k, f], partner)

    def r2_copy(k, f):
        return remote(s1.at[k, f], r2.at[k, f], r2_send.at[k, f], r2_recv.at[k, f], flip(me, ORDERS[k][1]))

    def r3_copy(k):
        return remote(s1.at[k, 2], r3.at[k], r3_send.at[k], r3_recv.at[k], flip(me, ORDERS[k][2]))

    for f in range(4):
        for k in range(3):
            pltpu.make_async_copy(emb.at[pl.ds(0, RS_TILES)], own.at[k, f], own_sem.at[k, f]).wait()
            for slot in (2, 0, 1):
                r1_copy(slot, k, f).wait_recv()

            def add_four(t, _, k=k, f=f):
                s1[k, f, t] = ((own[k, f, t].astype(jnp.float32) + r1[2, k, f, t].astype(jnp.float32))
                               + (r1[0, k, f, t].astype(jnp.float32) + r1[1, k, f, t].astype(jnp.float32)))
                return 0

            lax.fori_loop(0, RS_TILES, add_four, 0, unroll=2)
            if f < 2:
                r2_copy(k, f).start()
    for f in range(2):
        for k in range(3):
            r2_copy(k, f).wait_recv()

            def add_two(t, _, k=k, f=f):
                s1[k, 2 + f, t] = s1[k, 2 + f, t] + r2[k, f, t]
                return 0

            lax.fori_loop(0, RS_TILES, add_two, 0, unroll=2)
            if f == 0:
                r3_copy(k).start()

    shift = LEAD - (SHARD_ROWS * me - TILE_ROWS * rs_start(me))
    for k in range(3):
        r3_copy(k).wait_recv()

        def finish(t, _, k=k):
            total = (s1[k, 3, t] + r3[k, t]) * (1.0 / DEVS)
            row = shift + TILE_ROWS * (k * RS_TILES + t)
            for j in range(WIDTH // 128):
                grad[pl.ds(row + j, 8, stride=WIDTH // 128), :] = total[:, 128 * j:128 * (j + 1)]
            return 0

        lax.fori_loop(0, RS_TILES, finish, 0, unroll=2)

    def squares(i, acc):
        part = grad[pl.ds(pl.multiple_of(LEAD + i * 40, 8), 40), :]
        return acc + part * part

    acc = lax.fori_loop(0, 153, squares, jnp.zeros((40, 128), jnp.float32), unroll=3)
    nsend[...] = acc[0:8] + acc[8:16] + acc[16:24] + acc[24:32] + acc[32:40]
    for row in (6120, 6128, 6136):
        part = grad[pl.ds(LEAD + row, 8), :]
        nsend[...] = nsend[...] + part * part
    part = grad[pl.ds(LEAD + 6144, 5), :]
    nsend[0:5, :] = nsend[0:5, :] + part * part

    def n_copy(j):
        return remote(nsend, nrecv.at[me], n_send.at[j], n_recv.at[me], lax.rem(me + j, DEVS))

    for j in range(1, DEVS):
        n_copy(j).start()

    def full(value):
        return jnp.full((8, 128), value, jnp.float32)

    learn_rate, beta_one, beta_two, decay, max_norm = [full(hyp[i]) for i in range(5)]
    rest_one, rest_two = 1.0 - beta_one, 1.0 - beta_two
    hat_one = 1.0 / (1.0 - lax.integer_pow(beta_one, ADAM_STEP))
    hat_two = 1.0 / (1.0 - lax.integer_pow(beta_two, ADAM_STEP))
    for copy in state:
        copy.wait()
    for copy in ext_copies:
        copy.wait_recv()

    for j in range(1, DEVS):
        n_copy(j).wait_send()
        source = lax.rem(me + DEVS - j, DEVS)
        remote(nsend, nrecv.at[source], n_send.at[j], n_recv.at[source], partner).wait_recv()
    nrecv[me] = nsend[...]
    total = nrecv[0]
    for j in range(1, DEVS):
        total = total + nrecv[j]
    total = jnp.sum(jnp.sum(total, axis=1, keepdims=True), axis=0, keepdims=True)
    clip = jnp.minimum(1.0, max_norm / (jnp.sqrt(jnp.broadcast_to(total, (8, 128))) + CLIP_EPS))

    def wide(value, rows):
        if rows <= 8:
            return value[:rows]
        return jnp.concatenate([value] * (rows // 8), axis=0)

    def adam(g, m, v, p, first_row, rows):
        clipped = g * wide(clip, rows)
        m = wide(beta_one, rows) * m + wide(rest_one, rows) * clipped
        v = wide(beta_two, rows) * v + wide(rest_two, rows) * (clipped * clipped)
        index = first_row + lax.broadcasted_iota(jnp.int32, (rows, 128), 0)
        update = (m * wide(hat_one, rows)) / (jnp.sqrt(v * wide(hat_two, rows)) + ADAM_EPS)
        update = update + jnp.where(index < DECAY_ROWS, wide(decay, rows) * p, 0.0)
        return m, v, p - wide(learn_rate, rows) * update

    def adam_rows(row, rows):
        at = pl.ds(row, rows)
        shifted = pl.ds(row + LEAD, rows)
        m, v, p = adam(grad[shifted, :], mom[at, :], vel[at, :], par[at, :], SHARD_ROWS * me + row, rows)
        mom[at, :] = m
        vel[at, :] = v
        par[at, :] = p
        grad[shifted, :] = p

    def adam_block(i, _):
        adam_rows(pl.multiple_of(i * 40, 8), 40)
        return 0

    def ag_sizes(owner, k, run):
        if k < 2:
            run(AG_TILES)
            return
        longer = ag_start(owner + 1) - ag_start(owner) == 3 * AG_TILES + 1

        @pl.when(longer)
        def _():
            run(AG_TILES + 1)

        @pl.when(jnp.logical_not(longer))
        def _():
            run(AG_TILES)

    def ag_each(k, mask, run, dev=me):
        owner = flip_mask(dev, ORDERS[k], mask)
        first = ag_start(owner) + k * AG_TILES
        ag_sizes(owner, k, lambda size: run(vout.at[pl.ds(first, size)], size))

    def ag_link(k, mask, link):
        dev = flip(me, ORDERS[k][link])
        slot = mask + (1 << link)

        def copy(dst, size):
            src = stage.at[k, pl.ds(0, size)] if mask == 0 else dst
            return remote(src, dst, ag_send.at[k, slot], ag_recv.at[k, slot], dev)

        ag_each(k, mask, lambda dst, size: copy(dst, size).start())
        pending.append(lambda: ag_each(k, mask, lambda dst, size: copy(dst, size).wait_send()))

    def ag_across(k, mask):
        def copy(dst, size):
            src = stage.at[k, pl.ds(0, size)] if mask == 0 else dst
            return remote(src, dst, d2d_send.at[k, mask], d2d_recv.at[k, mask], partner)

        ag_each(k, mask, lambda dst, size: copy(dst, size).start())
        pending.append(lambda: ag_each(k, mask, lambda dst, size: copy(dst, size).wait_send()))

    def ag_arrived(k, mask):
        ag_each(k, mask, lambda dst, size: remote(
            dst, dst, ag_send.at[k, mask], ag_recv.at[k, mask], partner).wait_recv())

    pending = []
    bounds = ((0, 52), (52, 103), (103, 153))
    base = LEAD + TILE_ROWS * ag_start(me) - SHARD_ROWS * me
    for k in range(3):
        lax.fori_loop(bounds[k][0], bounds[k][1], adam_block, 0, unroll=1)
        if k == 2:
            adam_rows(6120, 24)
            adam_rows(6144, 5)
            at = pl.ds(LEAD + SHARD_ROWS, 40)
            _, _, p = adam(grad[at, :], ext[0], ext[1], ext[2], SHARD_ROWS * (me + 1), 40)
            grad[at, :] = p

        def pack(t, _, k=k):
            row = base + TILE_ROWS * (k * AG_TILES + t)
            for j in range(WIDTH // 128):
                stage[k, t, :, 128 * j:128 * (j + 1)] = grad[
                    pl.ds(row + j, 8, stride=WIDTH // 128), :].astype(jnp.bfloat16)
            return 0

        lax.fori_loop(0, AG_TILES + (1 if k == 2 else 0), pack, 0, unroll=1)
        ag_link(k, 0, 0)
    for k in range(3):
        ag_link(k, 0, 1)
    for k in range(3):
        ag_link(k, 0, 2)
    results = [pltpu.make_async_copy(src, dst, st_sem.at[i])
               for i, (src, dst) in enumerate(((mom, m_out), (vel, v_out), (par, p_out)))]
    for copy in results:
        copy.start()

    def ag_local(k):
        return lambda dst, size: pltpu.make_async_copy(stage.at[k, pl.ds(0, size)], dst, loc_sem.at[k])

    for k in range(3):
        ag_across(k, 0)
        ag_each(k, 0, lambda dst, size, k=k: ag_local(k)(dst, size).start())
    for k in range(3):
        ag_arrived(k, 1)
        ag_link(k, 1, 1)
        ag_across(k, 1)
    for k in range(3):
        ag_link(k, 1, 2)
    for k in range(3):
        ag_arrived(k, 2)
        ag_link(k, 2, 2)
        ag_across(k, 2)
    for k in range(3):
        ag_arrived(k, 4)
        ag_across(k, 4)
    for k in range(3):
        ag_arrived(k, 3)
        ag_link(k, 3, 2)
        ag_across(k, 3)
    for mask in (5, 6, 7):
        for k in range(3):
            ag_arrived(k, mask)
            ag_across(k, mask)
    for k in range(3):
        ag_each(k, 0, lambda dst, size, k=k: ag_local(k)(dst, size).wait())
    for mask in range(8):
        for k in range(3):
            ag_each(k, mask, lambda dst, size, k=k, mask=mask: remote(
                dst, dst, d2d_send.at[k, mask], d2d_recv.at[k, mask], partner).wait_recv(), partner)
    for wait in pending:
        wait()
    for copy in results:
        copy.wait()
    for copy in ext_copies:
        copy.wait_send()
    for f in range(4):
        for k in range(3):
            for slot in range(3):
                r1_copy(slot, k, f).wait_send()
            if f < 2:
                r2_copy(k, f).wait_send()
    for k in range(3):
        r3_copy(k).wait_send()


def solution(mesh):
    def local_update(*arrays):
        grads = arrays[:GRAD_COUNT]
        state = [arr.reshape(SHARD_ROWS, 128) for arr in arrays[GRAD_COUNT:GRAD_COUNT + 3]]
        shapes = [grad_arr.shape[1:] for grad_arr in grads]
        sizes = [math.prod(tensor_dims) for tensor_dims in shapes]
        emb = grads[0].reshape(EMBED_TILES, 8, WIDTH)
        tail_len = (TAIL_TILES + TAIL_START - EMBED_TILES) * 8 * WIDTH
        flat = [grad_arr.reshape(-1) for grad_arr in grads[1:]]
        flat.append(jnp.zeros((tail_len - sum(sizes[1:]),), jnp.bfloat16))
        tail = jnp.concatenate(flat).reshape(-1, 8, WIDTH)
        tail = jnp.concatenate([emb[TAIL_START:], tail], axis=0)
        any_spec = pl.BlockSpec(memory_space=pl.ANY)
        dma = pltpu.SemaphoreType.DMA
        bf16, f32 = jnp.bfloat16, jnp.float32
        vout, first, second, master = pl.pallas_call(
            kernel,
            out_shape=[jax.ShapeDtypeStruct((ALL_TILES, 8, WIDTH), bf16)]
            + [jax.ShapeDtypeStruct((SHARD_ROWS, 128), f32)] * 3,
            in_specs=[any_spec] * 5 + [pl.BlockSpec(memory_space=pltpu.SMEM)],
            out_specs=[any_spec] * 4,
            scratch_shapes=[
                pltpu.VMEM((3, 4, RS_TILES, 8, WIDTH), bf16),
                pltpu.VMEM((3, 3, 4, RS_TILES, 8, WIDTH), bf16),
                pltpu.VMEM((3, 4, RS_TILES, 8, WIDTH), f32),
                pltpu.VMEM((3, 2, RS_TILES, 8, WIDTH), f32),
                pltpu.VMEM((3, RS_TILES, 8, WIDTH), f32),
                pltpu.VMEM((SHARD_ROWS, 128), f32),
                pltpu.VMEM((SHARD_ROWS, 128), f32),
                pltpu.VMEM((SHARD_ROWS, 128), f32),
                pltpu.VMEM((3, TILE_ROWS, 128), f32),
                pltpu.VMEM((G_ROWS, 128), f32),
                pltpu.VMEM((3, AG_TILES + 1, 8, WIDTH), bf16),
                pltpu.VMEM((8, 128), f32),
                pltpu.VMEM((DEVS, 8, 128), f32),
                dma((3, 4)), dma((3, 3, 4)), dma((3, 3, 4)), dma((3, 2)), dma((3, 2)), dma((3,)), dma((3,)),
                dma((3,)), dma((3,)), dma((3,)), dma((DEVS,)), dma((DEVS,)),
                dma((3, 8)), dma((3, 8)), dma((3, 8)), dma((3, 8)), dma((3,)),
            ],
            compiler_params=pltpu.CompilerParams(
                collective_id=0, has_side_effects=True, vmem_limit_bytes=66_500_000),
        )(emb, tail, *state, arrays[GRAD_COUNT + 3])
        outs = [vout[:EMBED_TILES].reshape(shapes[0])]
        flat = vout[EMBED_TILES:].reshape(-1)
        start = 0
        for dims, size in zip(shapes[1:], sizes[1:]):
            outs.append(flat[start:start + size].reshape(dims))
            start += size
        return tuple(outs) + tuple(arr.reshape(-1) for arr in (first, second, master))

    in_specs = tuple([P("dp")] * GRAD_COUNT + [P("dp"), P("dp"), P("dp"), P()])
    out_specs = tuple([P()] * GRAD_COUNT + [P("dp"), P("dp"), P("dp")])
    return jax.shard_map(local_update, mesh=mesh, in_specs=in_specs, out_specs=out_specs, check_vma=False)
```

time: 1840 us -> 357 us (0.19)
  local copies, waits for them, and re-layouts: 705 us -> 85.8 us
  other arithmetic: 575 us -> 4.96 us
  waiting for transfers between devices: 486 us -> 0 us
  Pallas kernels: 0 us -> 264 us
  blocking collectives: 35.2 us -> 0 us
  between operations: 21.3 us -> 0.74 us
    unnamed x76 -> x29, local copies, waits for them, and re-layouts: 606 us -> 24.9 us
    all_to_all x1 -> x0, waiting for transfers between devices: 298 us -> none  [local_update(): received = lax.all_to_all(local_vec, 'dp', 0, 0, tiled=True)]
    pallas_call x0 -> x1, Pallas kernels: none -> 264 us  [local_update(): pl.pallas_call(kernel, out_shape=[jax.ShapeDtypeStruct((ALL_TILES, 8, WID...]
    reduce_sum x2 -> x0, other arithmetic: 262 us -> none  [the longest x1 261 us: local_update(): grad_part = jnp.sum(received, axis=0, dtype=jnp.float32) / group_size]
    all_gather x1 -> x0, waiting for transfers between devices: 188 us -> none  [local_update(): full_vec = lax.all_gather(new_master.astype(jnp.bfloat16), 'dp', tiled=True)]
    all_to_all x1 -> x0, other arithmetic: 152 us -> none  [local_update(): received = lax.all_to_all(local_vec, 'dp', 0, 0, tiled=True)]
    all_gather x1 -> x0, other arithmetic: 151 us -> none  [local_update(): full_vec = lax.all_gather(new_master.astype(jnp.bfloat16), 'dp', tiled=True)]
    reshape x14, local copies, waits for them, and re-layouts: 77.8 us -> 36.7 us  [the longest x1 17.1 us: local_update(): outs = [vout[:EMBED_TILES].reshape(shapes[0])]]
  transfers between devices with their start and end apart: 2 -> 0, of which waited for: 2 -> 0; matrix products, arithmetic and copies ran while one was open for 0% -> 0% of each run, Pallas kernels for 0% -> 0%
where the time goes in v1:
time: 357 us; the launch traced here: 356 us
  Pallas kernels  264 us (74%)
  local copies, waits for them, and re-layouts  85.8 us (24%)
  other arithmetic  4.96 us (1%)
    pallas_call x1, Pallas kernels, local_update(): pl.pallas_call(kernel, out_shape=[jax.ShapeDtypeStruct((ALL_TILES, 8, WID...  264 us
    unnamed x29, local copies, waits for them, and re-layouts  24.9 us
    slice x6, local copies, waits for them, and re-layouts, local_update(): outs.append(flat[start:start + size].reshape(dims))  17.8 us
    reshape x1, local copies, waits for them, and re-layouts, local_update(): outs = [vout[:EMBED_TILES].reshape(shapes[0])]  17.1 us
    reshape x1, local copies, waits for them, and re-layouts, local_update(): tail = jnp.concatenate(flat).reshape(-1, 8, WIDTH)  7.81 us

profile of v1, /device:TPU:0, one launch (start us, length us, event | category | flops | bytes accessed | tf_op | source)
XLA Modules:
  0.0 355.6 jit_solution(1790716027359446133)
XLA Ops:
  2.1 1.4 reshape.129
  3.5 1.2 slice_bitcast_fusion.1
  4.7 1.5 copy.30
  6.6 1.4 copy.31
  8.0 1.3 reshape.127
  9.3 1.4 copy.32
  10.7 1.3 reshape.128
  12.7 0.8 constant_dynamic-update-slice_fusion.8
  13.5 1.6 constant_dynamic-update-slice_fusion.7
  15.1 1.6 constant_dynamic-update-slice_fusion.6
  17.4 2.2 constant_dynamic-update-slice_fusion.4
  19.6 1.0 constant_dynamic-update-slice_fusion.3
  20.7 1.0 constant_dynamic-update-slice_fusion.2
  23.5 7.8 %reshape.135 = bf16[413,8,640]{2,1,0:T(8,128)(2,1)} reshape(bf16[2114560]{0:T(1024)(128)(2,1)} %broadcast_dynamic-update-slice_fusion) | data formatting | bytes 8458240 | tf_op jit(solution)/shard_map/reshape | solution.py:353
  31.3 5.0 %pad_maximum_fusion.tail = bf16[463,8,640]{2,1,0:T(8,128)(2,1)} fusion(bf16[413,8,640]{2,1,0:T(8,128)(2,1)} %reshape.135, bf16[50,8,640]{2,1,0:T(8,128)(2,1)S(1)} %slice_bitcast_fusion.1), kind=kLoop, calls=%fused_computation.1 | loop fusion | flops 2370560 | bytes 9482240 | tf_op jit(solution)/shard_map/concatenate | solution.py:354
  36.2 264.1 %shard_map.237 = (bf16[2460,8,640]{2,1,0:T(8,128)(2,1)}, f32[6149,128]{1,0:T(8,128)}, f32[6149,128]{1,0:T(8,128)}, f32[6149,128]{1,0:T(8,128)}) custom-call(bf16[2048,8,640]{2,1,0:T(8,128)(2,1)} %bitcast.27, bf16[463,8,640]{2,1,0:T(8,128)(2,1)} %pad_maximum_fusion.tail, f32[6149,128]{1,0:T(8,128)} %bitcast.31, f32[6149,128]{1,0:T(8,128)} %bitcast.32, ...), custom_call_target="tpu_custom_call" | custom-call | tf_op jit(solution)/shard_map/pallas_call | solution.py:358
  301.8 1.0 fusion.2
  303.5 1.0 copy.35
  305.1 1.0 copy.34
  306.1 2.0 fusion.1
  308.7 1.1 copy.33
  309.8 3.0 fusion
  312.8 1.6 reshape.145
  314.5 1.6 reshape.144
  316.1 4.5 %slice.69 = bf16[412,8,640]{2,1,0:T(8,128)(2,1)} slice(bf16[2460,8,640]{2,1,0:T(8,128)(2,1)} %get-tuple-element.17), slice={[2048:2460], [0:8], [0:640]} | slice | bytes 8437760 | tf_op jit(solution)/shard_map/slice | solution.py:386
  320.6 17.1 %slice_bitcast_fusion = bf16[16384,640]{1,0:T(8,128)(2,1)} fusion(bf16[2460,8,640]{2,1,0:T(8,128)(2,1)} %get-tuple-element.17), kind=kLoop, calls=%fused_computation | loop fusion | bytes 41943040 | tf_op jit(solution)/shard_map/reshape | solution.py:385
  337.8 9.6 %slice.70 = bf16[4120,2,256]{2,1,0:T(2,128)(2,1)} reshape(bf16[412,8,640]{2,1,0:T(8,128)(2,1)} %slice.69) | data formatting | bytes 8437760 | tf_op jit(solution)/shard_map/slice | solution.py:389
  347.4 1.4 slice.72
  348.9 1.9 copy.49
  350.7 1.9 copy.50
  352.6 1.2 copy-done
  353.8 1.9 copy.51
  (22 shorter events, 8.6 us)
Async XLA Ops:
  3.5 8.5 %copy-start.3 = (bf16[1,6,128,640]{3,2,1,0:T(8,128)(2,1)S(1)}, bf16[1,6,128,640]{3,2,1,0:T(8,128)(2,1)}, u32[]{:S(2)}) copy-start(bf16[1,6,128,640]{3,2,1,0:T(8,128)(2,1)} %param.21) | copy-start | bytes 2949124
  12.7 7.0 %copy-start.4 = (bf16[1,6,640,128]{3,2,1,0:T(8,128)(2,1)S(1)}, bf16[1,6,640,128]{3,2,1,0:T(8,128)(2,1)}, u32[]{:S(2)}) copy-start(bf16[1,6,640,128]{3,2,1,0:T(8,128)(2,1)} %param.20) | copy-start | bytes 2949124
  337.8 11.1 %copy-start.2 = (f32[6149,128]{1,0:T(8,128)S(1)}, f32[6149,128]{1,0:T(8,128)}, u32[]{:S(2)}) copy-start(f32[6149,128]{1,0:T(8,128)} %get-tuple-element.18) | copy-start | bytes 9444868
  347.4 3.3 copy-start.1
  350.7 3.0 copy-start

commit v2 on v1

v2 whole, which is shorter than its diff:
```python
import functools
import math
import jax
import jax.numpy as jnp
from jax import lax
from jax.experimental import pallas as pl
from jax.experimental.pallas import tpu as pltpu
from jax.sharding import PartitionSpec as P

ADAM_STEP = 7
ADAM_EPS = 1e-8
CLIP_EPS = 1e-6
GRAD_COUNT = 10
MESH = pl.DeviceIdType.MESH

DEVS = 16
OTHERS = range(1, DEVS)
THIRDS = range(3)
PAIR = range(2)
LANES = 128
WIDTH = 640
SHARD_ROWS = 6149
TILE_ROWS = 40
EMBED_TILES = 2048
ALL_TILES = 2460
DECAY_ROWS = 98240
FIRST_TAIL = 13
TAIL_START = (SHARD_ROWS * FIRST_TAIL) // TILE_ROWS
RS_TILES = 52
TAIL_TILES = (SHARD_ROWS * 15) // TILE_ROWS + 3 * RS_TILES - TAIL_START
AG_TILES = 51
LEAD = 40
G_ROWS = LEAD + 3 * RS_TILES * TILE_ROWS
ORDERS = ((2, 4, 8), (4, 8, 2), (8, 2, 4))


def flip(dev, stride):
    return dev + stride - 2 * stride * lax.rem(dev // stride, 2)


def rs_start(dev):
    return (SHARD_ROWS * dev) // TILE_ROWS


def ag_start(dev):
    return (SHARD_ROWS * dev + TILE_ROWS - 1) // TILE_ROWS


def flip_mask(dev, order, mask):
    for bit, stride in enumerate(order):
        if mask >> bit & 1:
            dev = flip(dev, stride)
    return dev


SMALL = {}
for _name, _tiles in (("q", 48), ("k", 12), ("v", 12), ("out", 48), ("gate", 96), ("up", 96),
                      ("down", 96), ("norms", 3), ("qk", 1)):
    SMALL[_name] = (EMBED_TILES if not SMALL else sum(SMALL[_last]), _tiles)
    _last = _name
LAYERS = 6
COLS = WIDTH // LANES
OUT_TILES = 48 * RS_TILES
SPARE = 42 * RS_TILES
PIECE_ROWS = RS_TILES * TILE_ROWS


def slot_tiles(slot, k, f):
    index = 36 + f * 3 + k if slot == 3 else (slot * 3 + k) * 4 + f
    return pl.ds(index * RS_TILES, RS_TILES)


def sum_rows(k, f):
    return pl.ds((f * 3 + k) * PIECE_ROWS, PIECE_ROWS)


def put_tile(dst, tile, rows, first, stride):
    for j in range(COLS):
        dst[tile, :, LANES * j:LANES * (j + 1)] = rows[pl.ds(first + j, 8, stride=stride), :].astype(jnp.bfloat16)


def pack_wide(src, dst, first_tile, rows, tiles):
    def step(i, _):
        rows[pl.ds(pl.multiple_of(i * 80, 16), 80), :] = src[pl.ds(pl.multiple_of(i * 80, 16), 80), :].astype(jnp.float32)
        for half in PAIR:
            put_tile(dst, first_tile + 2 * i + half, rows, i * 80 + half * 40, COLS)
        return 0

    lax.fori_loop(0, tiles // 2, step, 0)


def pack_narrow(src, dst, first_tile, rows, width):
    folds = LANES // width
    lane = lax.broadcasted_iota(jnp.int32, (8, LANES), 1) // width
    for layer in range(LAYERS):
        block = src[pl.ds(layer * width // 8, width // 8)].astype(jnp.float32).reshape(width, WIDTH)
        rows[pl.ds(layer * WIDTH, WIDTH), :] = jnp.concatenate([block] * folds, axis=0).T
    tiles = LAYERS * width // 8

    def step(t, _):
        for j in range(COLS):
            first = folds * (40 * t + j)
            value = rows[pl.ds(first, 8, stride=folds * COLS), :]
            for fold in range(1, folds):
                value = jnp.where(lane == fold, rows[pl.ds(first + fold, 8, stride=folds * COLS), :], value)
            dst[first_tile + t, :, LANES * j:LANES * (j + 1)] = value.astype(jnp.bfloat16)
        return 0

    lax.fori_loop(0, tiles, step, 0)


def unpack_wide(src, first_tile, dst, rows, tiles):
    def step(i, _):
        for half in PAIR:
            for j in range(COLS):
                rows[pl.ds(i * 80 + half * 40 + j, 8, stride=COLS), :] = src[
                    first_tile + 2 * i + half, :, LANES * j:LANES * (j + 1)].astype(jnp.float32)
        dst[pl.ds(pl.multiple_of(i * 80, 16), 80), :] = rows[pl.ds(pl.multiple_of(i * 80, 16), 80), :].astype(jnp.bfloat16)
        return 0

    lax.fori_loop(0, tiles // 2, step, 0)


def unpack_narrow(src, first_tile, dst, rows, width):
    folds = LANES // width
    tiles = LAYERS * width // 8

    def step(t, _):
        for j in range(COLS):
            value = src[first_tile + t, :, LANES * j:LANES * (j + 1)].astype(jnp.float32)
            for fold in range(folds):
                turned = value if fold == 0 else pltpu.roll(value, LANES - fold * width, 1)
                rows[pl.ds(folds * (40 * t + j) + fold, 8, stride=folds * COLS), :] = turned
        return 0

    lax.fori_loop(0, tiles, step, 0)
    for layer in range(LAYERS):
        block = rows[pl.ds(layer * WIDTH, WIDTH), :].T[:width]
        dst[pl.ds(layer * width // 8, width // 8)] = block.reshape(width // 8, 8, WIDTH).astype(jnp.bfloat16)


def kernel(emb, gq, gk, gv, go, gg, gu, gd, gn, gqk, m_in, v_in, p_in, hyp, mom, vel, par, vout, tail,
           s1, r2, r3, ext, nsend, nrecv, wide_raw, q_raw, k_raw, v_raw, n_raw, qk_raw, n_tiles,
           raw_sem, relay_sem, tail_sem,
           own_sem, r1_send, r1_recv, r2_send, r2_recv, r3_send, r3_recv, st_sem,
           ext_send, ext_recv, n_send, n_recv, ag_send, ag_recv, d2d_send, d2d_recv):
    grad = s1.at[pl.ds(0, G_ROWS)]
    me = lax.axis_index("dp")
    partner = flip(me, 1)

    def remote(src, dst, ssem, rsem, dev):
        return pltpu.make_async_remote_copy(
            src_ref=src, dst_ref=dst, send_sem=ssem, recv_sem=rsem, device_id=(dev,), device_id_type=MESH)

    def from_shard(owner, k, make, embed=True, small=True):
        first = rs_start(owner) + k * RS_TILES

        if embed:
            @pl.when(owner < FIRST_TAIL)
            def _():
                make(emb.at[pl.ds(first, RS_TILES)]).start()

        if small:
            @pl.when(owner >= FIRST_TAIL)
            def _():
                make(tail.at[pl.ds(first - TAIL_START, RS_TILES)]).start()

    def rs_owner(dev, k, f):
        return flip_mask(dev, ORDERS[k], (0 if f >= 2 else 2) + (4 if f % 2 == 0 else 0))

    state = [pltpu.make_async_copy(src, dst, st_sem.at[i])
             for i, (src, dst) in enumerate(((m_in, mom), (v_in, vel), (p_in, par)))]

    def load_own(f, embed=True, small=True):
        for k in THIRDS:
            from_shard(rs_owner(me, k, f), k, lambda src, k=k: pltpu.make_async_copy(
                src, vout.at[slot_tiles(3, k, f)], own_sem.at[k, f]), embed, small)

    def send_first(f, embed=True, small=True):
        for k in THIRDS:
            for slot in THIRDS:
                dev = partner if slot == 2 else flip(me, ORDERS[k][0])
                if slot == 1:
                    dev = flip(dev, 1)
                from_shard(rs_owner(dev, k, f), k, lambda src, k=k, slot=slot, dev=dev: remote(
                    src, vout.at[slot_tiles(slot, k, f)], r1_send.at[slot, k, f], r1_recv.at[slot, k, f], dev),
                    embed, small)

    raw = [pltpu.make_async_copy(src, dst, raw_sem.at[i]) for i, (src, dst) in enumerate((
        (gg, wide_raw.at[0]), (gu, wide_raw.at[1]), (gq, q_raw), (gk, k_raw), (gv, v_raw), (gn, n_raw), (gqk, qk_raw)))]
    for copy in raw:
        copy.start()
    edge = EMBED_TILES - TAIL_START
    relayed = []
    start = SPARE
    for i, (src, first, tiles) in enumerate(((go, SMALL["out"][0], 48), (gd, SMALL["down"][0], 96),
                                             (emb.at[pl.ds(TAIL_START, edge)], TAIL_START, edge))):
        part = vout.at[pl.ds(start, tiles)]
        copy = pltpu.make_async_copy(src, part, relay_sem.at[i])
        copy.start()
        relayed.append((copy, pltpu.make_async_copy(part, tail.at[pl.ds(first - TAIL_START, tiles)], tail_sem.at[i])))
        start += tiles
    for f in PAIR:
        load_own(f, small=False)
    barrier = pltpu.get_barrier_semaphore()
    for j in OTHERS:
        pl.semaphore_signal(barrier, inc=1, device_id=(lax.rem(me + j, DEVS),), device_id_type=MESH)
    pl.semaphore_wait(barrier, DEVS - 1)
    for f in PAIR:
        send_first(f, small=False)

    for copy, onward in relayed:
        copy.wait()
        onward.start()
    onwards = [onward for _, onward in relayed]

    raw_names = list(SMALL)

    def to_tail(src, name):
        first, tiles = SMALL[name]
        copy = pltpu.make_async_copy(src, tail.at[pl.ds(first - TAIL_START, tiles)], tail_sem.at[3 + raw_names.index(name)])
        copy.start()
        onwards.append(copy)

    spare = start
    for i, name in enumerate(("gate", "up")):
        raw[i].wait()
        pack_wide(wide_raw.at[i], vout, spare, grad, 96)
        to_tail(vout.at[pl.ds(spare, 96)], name)
        onwards.pop().wait()
    for i, (name, src, width) in enumerate((("q", q_raw, 64), ("k", k_raw, 16), ("v", v_raw, 16))):
        raw[2 + i].wait()
        pack_narrow(src, vout, spare, grad, width)
        tiles = SMALL[name][1]
        to_tail(vout.at[pl.ds(spare, tiles)], name)
        spare += tiles
    raw[5].wait()
    raw[6].wait()
    for i in THIRDS:
        n_tiles[i] = jnp.concatenate([n_raw[2 * i].astype(jnp.float32), n_raw[2 * i + 1].astype(jnp.float32)],
                                     axis=0).astype(jnp.bfloat16)
    grad[24:40, :] = jnp.zeros((16, LANES), jnp.float32)
    for layer in range(LAYERS):
        pair = qk_raw[layer].astype(jnp.float32)
        for i in PAIR:
            for half in PAIR:
                row = (2 * layer + i) * 2 + half
                grad[row:row + 1, :] = pair[i:i + 1, LANES * half:LANES * (half + 1)]
    put_tile(n_tiles, 3, grad, 0, COLS)
    to_tail(n_tiles.at[pl.ds(0, 3)], "norms")
    to_tail(n_tiles.at[pl.ds(3, 1)], "qk")
    for copy in onwards:
        copy.wait()
    for f in PAIR:
        send_first(f, embed=False)
        load_own(f, embed=False)
    for f in range(2, 4):
        send_first(f)
        load_own(f)
    before = lax.rem(me + DEVS - 1, DEVS)
    ext_copies = [remote(src.at[pl.ds(0, TILE_ROWS)], ext.at[i], ext_send.at[i], ext_recv.at[i], before)
                  for i, src in enumerate((m_in, v_in, p_in))]
    for copy in ext_copies:
        copy.start()
    for copy in state:
        copy.start()

    def r1_copy(slot, k, f):
        return remote(emb.at[pl.ds(0, RS_TILES)], vout.at[slot_tiles(slot, k, f)], r1_send.at[slot, k, f],
                      r1_recv.at[slot, k, f], partner)

    def r2_copy(k, f):
        return remote(s1.at[sum_rows(k, f)], r2.at[k, f], r2_send.at[k, f], r2_recv.at[k, f], flip(me, ORDERS[k][1]))

    def r3_copy(k):
        return remote(s1.at[sum_rows(k, 2)], r3.at[k], r3_send.at[k], r3_recv.at[k], flip(me, ORDERS[k][2]))

    for f in range(4):
        for k in THIRDS:
            pltpu.make_async_copy(
                emb.at[pl.ds(0, RS_TILES)], vout.at[slot_tiles(3, k, f)], own_sem.at[k, f]).wait()
            for slot in (2, 0, 1):
                r1_copy(slot, k, f).wait_recv()

            def add_four(t, _, k=k, f=f):
                a, b, c, d = [vout[slot_tiles(slot, k, f).start + t].astype(jnp.float32) for slot in (3, 2, 0, 1)]
                total = (a + b) + (c + d)
                row = sum_rows(k, f).start + TILE_ROWS * t
                for j in range(COLS):
                    s1[pl.ds(pl.multiple_of(row + 8 * j, 8), 8), :] = total[:, LANES * j:LANES * (j + 1)]
                return 0

            lax.fori_loop(0, RS_TILES, add_four, 0, unroll=2)
            if f < 2:
                r2_copy(k, f).start()
    for f in PAIR:
        for k in THIRDS:
            r2_copy(k, f).wait_recv()

            def add_two(t, _, k=k, f=f):
                row = pl.multiple_of(TILE_ROWS * t, 8)
                at = pl.ds(pl.multiple_of(sum_rows(k, 2 + f).start + TILE_ROWS * t, 8), TILE_ROWS)
                s1[at, :] = s1[at, :] + r2[k, f, pl.ds(row, TILE_ROWS), :]
                return 0

            lax.fori_loop(0, RS_TILES, add_two, 0, unroll=2)
            if f == 0:
                r3_copy(k).start()

    shift = LEAD - (SHARD_ROWS * me - TILE_ROWS * rs_start(me))
    for k in THIRDS:
        for f in PAIR:
            r2_copy(k, f).wait_send()
    for k in THIRDS:
        r3_copy(k).wait_recv()

        def finish(t, _, k=k):
            row = pl.multiple_of(TILE_ROWS * t, 8)
            at = pl.ds(pl.multiple_of(sum_rows(k, 3).start + TILE_ROWS * t, 8), TILE_ROWS)
            total = (s1[at, :] + r3[k, pl.ds(row, TILE_ROWS), :]) * (1.0 / DEVS)
            row = shift + TILE_ROWS * (k * RS_TILES + t)
            for j in range(COLS):
                grad[pl.ds(row + j, 8, stride=COLS), :] = total[8 * j:8 * (j + 1), :]
            return 0

        lax.fori_loop(0, RS_TILES, finish, 0, unroll=2)

    def squares(i, acc):
        part = grad[pl.ds(pl.multiple_of(LEAD + i * 40, 8), 40), :]
        return acc + part * part

    acc = lax.fori_loop(0, 153, squares, jnp.zeros((40, LANES), jnp.float32), unroll=3)
    nsend[...] = acc[0:8] + acc[8:16] + acc[16:24] + acc[24:32] + acc[32:40]
    for row in (6120, 6128, 6136):
        part = grad[pl.ds(LEAD + row, 8), :]
        nsend[...] = nsend[...] + part * part
    part = grad[pl.ds(LEAD + 6144, 5), :]
    nsend[0:5, :] = nsend[0:5, :] + part * part

    def n_copy(j):
        return remote(nsend, nrecv.at[me], n_send.at[j], n_recv.at[me], lax.rem(me + j, DEVS))

    for j in OTHERS:
        n_copy(j).start()

    def full(value):
        return jnp.full((8, LANES), value, jnp.float32)

    learn_rate, beta_one, beta_two, decay, max_norm = [full(hyp[i]) for i in range(5)]
    rest_one, rest_two = 1.0 - beta_one, 1.0 - beta_two
    hat_one = 1.0 / (1.0 - lax.integer_pow(beta_one, ADAM_STEP))
    hat_two = 1.0 / (1.0 - lax.integer_pow(beta_two, ADAM_STEP))
    for copy in state:
        copy.wait()
    for copy in ext_copies:
        copy.wait_recv()

    for j in OTHERS:
        n_copy(j).wait_send()
        source = lax.rem(me + DEVS - j, DEVS)
        remote(nsend, nrecv.at[source], n_send.at[j], n_recv.at[source], partner).wait_recv()
    nrecv[me] = nsend[...]
    total = nrecv[0]
    for j in OTHERS:
        total = total + nrecv[j]
    total = jnp.sum(jnp.sum(total, axis=1, keepdims=True), axis=0, keepdims=True)
    clip = jnp.minimum(1.0, max_norm / (jnp.sqrt(jnp.broadcast_to(total, (8, LANES))) + CLIP_EPS))

    def wide(value, rows):
        if rows <= 8:
            return value[:rows]
        return jnp.concatenate([value] * (rows // 8), axis=0)

    def adam(g, m, v, p, first_row, rows):
        clipped = g * wide(clip, rows)
        m = wide(beta_one, rows) * m + wide(rest_one, rows) * clipped
        v = wide(beta_two, rows) * v + wide(rest_two, rows) * (clipped * clipped)
        index = first_row + lax.broadcasted_iota(jnp.int32, (rows, LANES), 0)
        update = (m * wide(hat_one, rows)) / (jnp.sqrt(v * wide(hat_two, rows)) + ADAM_EPS)
        update = update + jnp.where(index < DECAY_ROWS, wide(decay, rows) * p, 0.0)
        return m, v, p - wide(learn_rate, rows) * update

    def adam_rows(row, rows):
        at = pl.ds(row, rows)
        shifted = pl.ds(row + LEAD, rows)
        m, v, p = adam(grad[shifted, :], mom[at, :], vel[at, :], par[at, :], SHARD_ROWS * me + row, rows)
        mom[at, :] = m
        vel[at, :] = v
        par[at, :] = p
        grad[shifted, :] = p

    def adam_block(i, _):
        adam_rows(pl.multiple_of(i * 40, 8), 40)
        return 0

    def ag_sizes(owner, k, run):
        if k < 2:
            run(AG_TILES)
            return
        longer = ag_start(owner + 1) - ag_start(owner) == 3 * AG_TILES + 1

        @pl.when(longer)
        def _():
            run(AG_TILES + 1)

        @pl.when(jnp.logical_not(longer))
        def _():
            run(AG_TILES)

    def ag_each(k, mask, run, dev=me):
        owner = flip_mask(dev, ORDERS[k], mask)
        first = ag_start(owner) + k * AG_TILES
        ag_sizes(owner, k, lambda size: run(vout.at[pl.ds(first, size)], size))

    def ag_link(k, mask, link):
        dev = flip(me, ORDERS[k][link])
        slot = mask + (1 << link)

        def copy(dst, size):
            return remote(dst, dst, ag_send.at[k, slot], ag_recv.at[k, slot], dev)

        ag_each(k, mask, lambda dst, size: copy(dst, size).start())
        pending.append(lambda: ag_each(k, mask, lambda dst, size: copy(dst, size).wait_send()))

    def ag_across(k, mask):
        def copy(dst, size):
            return remote(dst, dst, d2d_send.at[k, mask], d2d_recv.at[k, mask], partner)

        ag_each(k, mask, lambda dst, size: copy(dst, size).start())
        pending.append(lambda: ag_each(k, mask, lambda dst, size: copy(dst, size).wait_send()))

    def ag_arrived(k, mask):
        ag_each(k, mask, lambda dst, size: remote(
            dst, dst, ag_send.at[k, mask], ag_recv.at[k, mask], partner).wait_recv())

    pending = []
    bounds = ((0, 52), (52, 103), (103, 153))
    base = LEAD + TILE_ROWS * ag_start(me) - SHARD_ROWS * me
    for k in THIRDS:
        lax.fori_loop(bounds[k][0], bounds[k][1], adam_block, 0, unroll=1)
        if k == 2:
            adam_rows(6120, 24)
            adam_rows(6144, 5)
            at = pl.ds(LEAD + SHARD_ROWS, 40)
            _, _, p = adam(grad[at, :], ext[0], ext[1], ext[2], SHARD_ROWS * (me + 1), 40)
            grad[at, :] = p

        first = ag_start(me) + k * AG_TILES

        def pack(t, _, k=k, first=first):
            put_tile(vout, first + t, grad, base + TILE_ROWS * (k * AG_TILES + t), COLS)
            return 0

        count = ag_start(me + 1) - first if k == 2 else AG_TILES
        lax.fori_loop(0, count, pack, 0)
        ag_link(k, 0, 0)
    for k in THIRDS:
        ag_link(k, 0, 1)
    for k in THIRDS:
        ag_link(k, 0, 2)
    for k in THIRDS:
        ag_across(k, 0)
    for k in THIRDS:
        ag_arrived(k, 1)
        ag_link(k, 1, 1)
        ag_across(k, 1)
    for k in THIRDS:
        ag_link(k, 1, 2)
    for k in THIRDS:
        ag_arrived(k, 2)
        ag_link(k, 2, 2)
        ag_across(k, 2)
    for k in THIRDS:
        ag_arrived(k, 4)
        ag_across(k, 4)
    for k in THIRDS:
        ag_arrived(k, 3)
        ag_link(k, 3, 2)
        ag_across(k, 3)
    for mask in (5, 6, 7):
        for k in THIRDS:
            ag_arrived(k, mask)
            ag_across(k, mask)
    for mask in range(8):
        for k in THIRDS:
            ag_each(k, mask, lambda dst, size, k=k, mask=mask: remote(
                dst, dst, d2d_send.at[k, mask], d2d_recv.at[k, mask], partner).wait_recv(), partner)
    for wait in pending:
        wait()
    for copy in ext_copies:
        copy.wait_send()
    for f in range(4):
        for k in THIRDS:
            for slot in THIRDS:
                r1_copy(slot, k, f).wait_send()
    for k in THIRDS:
        r3_copy(k).wait_send()


def flush(mom, vel, par, vout, embed, oq, ok, ov, oo, og, ou, od, on, oqk, m_out, v_out, p_out,
          rows, wide_out, q_out, k_out, v_new, n_out, qk_out, sem):
    copies = []

    def send(src, dst):
        copy = pltpu.make_async_copy(src, dst, sem.at[len(copies)])
        copy.start()
        copies.append(copy)

    for i in range(4):
        part = pl.ds(i * EMBED_TILES // 4, EMBED_TILES // 4)
        send(vout.at[part], embed.at[part])
    for src, dst in ((mom, m_out), (vel, v_out), (par, p_out)):
        send(src, dst)
    for name, dst in (("out", oo), ("down", od)):
        send(vout.at[pl.ds(*SMALL[name])], dst)
    for i, (name, dst) in enumerate((("gate", og), ("up", ou))):
        unpack_wide(vout, SMALL[name][0], wide_out.at[i], rows, 96)
        send(wide_out.at[i], dst)
    for name, block, dst, width in (("q", q_out, oq, 64), ("k", k_out, ok, 16), ("v", v_new, ov, 16)):
        unpack_narrow(vout, SMALL[name][0], block, rows, width)
        send(block, dst)
    for i in THIRDS:
        tile = vout[SMALL["norms"][0] + i].astype(jnp.float32)
        n_out[2 * i] = tile[0:4].astype(jnp.bfloat16)
        n_out[2 * i + 1] = tile[4:8].astype(jnp.bfloat16)
    send(n_out, on)
    for j in range(COLS):
        rows[pl.ds(j, 8, stride=COLS), :] = vout[SMALL["qk"][0], :, LANES * j:LANES * (j + 1)].astype(jnp.float32)
    for layer in range(LAYERS):
        four = rows[4 * layer:4 * layer + 4, :]
        pair = [jnp.concatenate([four[2 * i:2 * i + 1], four[2 * i + 1:2 * i + 2]], axis=1) for i in PAIR]
        qk_out[layer] = jnp.concatenate(pair, axis=0).astype(jnp.bfloat16)
    send(qk_out, oqk)
    for copy in copies:
        copy.wait()


def solution(mesh):
    def local_update(*arrays):
        grads = [arr.reshape(arr.shape[1:]) for arr in arrays[:GRAD_COUNT]]
        state = [arr.reshape(SHARD_ROWS, LANES) for arr in arrays[GRAD_COUNT:GRAD_COUNT + 3]]
        shapes = [grad_arr.shape for grad_arr in grads]
        any_spec = pl.BlockSpec(memory_space=pl.ANY)
        vmem_spec = pl.BlockSpec(memory_space=pltpu.VMEM)
        dma = pltpu.SemaphoreType.DMA
        bf16, f32 = jnp.bfloat16, jnp.float32
        tiled = []
        for i, grad_arr in enumerate(grads[:8]):
            if i in (1, 2, 3):
                grad_arr = jnp.swapaxes(grad_arr, 1, 2)
            tiled.append(grad_arr.reshape(-1, LANES) if i in (5, 6) else grad_arr.reshape(-1, 8, WIDTH))
        tiled += grads[8:]
        small = [jax.ShapeDtypeStruct(arr.shape, bf16) for arr in tiled[1:]]
        *kept, _ = pl.pallas_call(
            kernel,
            out_shape=[pltpu.VMEM((SHARD_ROWS, LANES), f32)] * 3
            + [pltpu.VMEM((OUT_TILES, 8, WIDTH), bf16)]
            + [pltpu.HBM((TAIL_TILES, 8, WIDTH), bf16)],
            in_specs=[any_spec] * 13 + [pl.BlockSpec(memory_space=pltpu.SMEM)],
            out_specs=[vmem_spec] * 4 + [any_spec],
            scratch_shapes=[
                pltpu.VMEM((3 * 4 * PIECE_ROWS, LANES), f32),
                pltpu.VMEM((3, 2, PIECE_ROWS, LANES), f32),
                pltpu.VMEM((3, PIECE_ROWS, LANES), f32),
                pltpu.VMEM((3, TILE_ROWS, LANES), f32),
                pltpu.VMEM((8, LANES), f32),
                pltpu.VMEM((DEVS, 8, LANES), f32),
                pltpu.VMEM((2, 3840, LANES), bf16),
                pltpu.VMEM((48, 8, WIDTH), bf16),
                pltpu.VMEM((12, 8, WIDTH), bf16),
                pltpu.VMEM((12, 8, WIDTH), bf16),
                pltpu.VMEM(shapes[8], bf16),
                pltpu.VMEM(shapes[9], bf16),
                pltpu.VMEM((4, 8, WIDTH), bf16),
                dma((7,)), dma((3,)), dma((3 + len(SMALL),)),
                dma((3, 4)), dma((3, 3, 4)), dma((3, 3, 4)), dma((3, 2)), dma((3, 2)), dma((3,)), dma((3,)),
                dma((3,)), dma((3,)), dma((3,)), dma((DEVS,)), dma((DEVS,)),
                dma((3, 8)), dma((3, 8)), dma((3, 8)), dma((3, 8)),
            ],
            compiler_params=pltpu.CompilerParams(
                collective_id=0, has_side_effects=True, vmem_limit_bytes=26_500_000),
        )(*tiled, *state, arrays[GRAD_COUNT + 3])
        kept = [pltpu.with_memory_space_constraint(arr, pltpu.VMEM) for arr in kept]
        outs = pl.pallas_call(
            flush,
            out_shape=[jax.ShapeDtypeStruct((EMBED_TILES, 8, WIDTH), bf16)] + small
            + [jax.ShapeDtypeStruct((SHARD_ROWS, LANES), f32)] * 3,
            in_specs=[vmem_spec] * 4,
            out_specs=[any_spec] * 13,
            scratch_shapes=[
                pltpu.VMEM((3840, LANES), f32),
                pltpu.VMEM((2, 3840, LANES), bf16),
                pltpu.VMEM((48, 8, WIDTH), bf16),
                pltpu.VMEM((12, 8, WIDTH), bf16),
                pltpu.VMEM((12, 8, WIDTH), bf16),
                pltpu.VMEM(shapes[8], bf16),
                pltpu.VMEM(shapes[9], bf16),
                dma((20,)),
            ],
            compiler_params=pltpu.CompilerParams(has_side_effects=True, vmem_limit_bytes=5_200_000),
        )(*kept)
        params = []
        for i, dims in enumerate(shapes):
            if i in (1, 2, 3):
                params.append(jnp.swapaxes(outs[i].reshape(dims[0], dims[2], dims[1]), 1, 2))
            else:
                params.append(outs[i].reshape(dims))
        return tuple(params) + tuple(arr.reshape(-1) for arr in outs[GRAD_COUNT:])

    in_specs = tuple([P("dp")] * GRAD_COUNT + [P("dp"), P("dp"), P("dp"), P()])
    out_specs = tuple([P()] * GRAD_COUNT + [P("dp"), P("dp"), P("dp")])
    return jax.shard_map(local_update, mesh=mesh, in_specs=in_specs, out_specs=out_specs, check_vma=False)
```

time: 357 us -> 277 us (0.78)
  local copies, waits for them, and re-layouts: 85.8 us -> 0 us
  Pallas kernels: 264 us -> 276 us
  other arithmetic: 4.96 us -> 0 us
    reshape x14 -> x0, local copies, waits for them, and re-layouts: 36.7 us -> none  [the longest x1 17.1 us: local_update(): outs = [vout[:EMBED_TILES].reshape(shapes[0])]]
    unnamed x29 -> x0, local copies, waits for them, and re-layouts: 24.9 us -> none
    slice x8 -> x0, local copies, waits for them, and re-layouts: 23.5 us -> none  [the longest x6 17.8 us: local_update(): outs.append(flat[start:start + size].reshape(dims))]
    pallas_call x1 -> x2, Pallas kernels: 264 us -> 276 us  [the longest x1 265 us: local_update(): pl.pallas_call(kernel, out_shape=[pltpu.VMEM((SHARD_ROWS, LANES), f32)] *...]
    concatenate x1 -> x0, other arithmetic: 4.96 us -> none  [local_update(): tail = jnp.concatenate([emb[TAIL_START:], tail], axis=0)]
where the time goes in v2:
time: 277 us
  Pallas kernels  276 us (100%)
    pallas_call x1, Pallas kernels, local_update(): pl.pallas_call(kernel, out_shape=[pltpu.VMEM((SHARD_ROWS, LANES), f32)] *...  265 us
    pallas_call x1, Pallas kernels, local_update(): pl.pallas_call(flush, out_shape=[jax.ShapeDtypeStruct((EMBED_TILES, 8, WI...  11.4 us

profile of v2, /device:TPU:0, one launch (start us, length us, event | category | flops | bytes accessed | tf_op | source)
XLA Modules:
  0.0 276.6 jit_solution(1662808028249979418)
XLA Ops:
  0.7 264.6 %shard_map.237 = (f32[6149,128]{1,0:T(8,128)S(1)}, f32[6149,128]{1,0:T(8,128)S(1)}, f32[6149,128]{1,0:T(8,128)S(1)}, bf16[2496,8,640]{2,1,0:T(8,128)(2,1)S(1)}, bf16[463,8,640]{2,1,0:T(8,128)(2,1)}) custom-call(bf16[2048,8,640]{2,1,0:T(8,128)(2,1)} %bitcast.42, bf16[48,8,640]{2,1,0:T(8,128)(2,1)} %bitcast.49, bf16[12,8,640]{2,1,0:T(8,128)(2,1)} %bitcast.51, ...), custom_call_target="tpu_custom_call" | custom-call | tf_op jit(solution)/shard_map/pallas_call | solution.py:554
  265.2 11.4 %shard_map.238 = (bf16[2048,8,640]{2,1,0:T(8,128)(2,1)}, bf16[48,8,640]{2,1,0:T(8,128)(2,1)}, bf16[12,8,640]{2,1,0:T(8,128)(2,1)}, bf16[12,8,640]{2,1,0:T(8,128)...) custom-call(f32[6149,128]{1,0:T(8,128)S(1)} %get-tuple-element.30.mo, ...), custom_call_target="tpu_custom_call" | custom-call | tf_op jit(solution)/shard_map/pallas_call | solution.py:584

commit v3 on v2

--- a/solution.py
+++ b/solution.py
@@ -186,6 +186,9 @@
                     src, vout.at[slot_tiles(slot, k, f)], r1_send.at[slot, k, f], r1_recv.at[slot, k, f], dev),
                     embed, small)
 
+    barrier = pltpu.get_barrier_semaphore()
+    for j in OTHERS:
+        pl.semaphore_signal(barrier, inc=1, device_id=(lax.rem(me + j, DEVS),), device_id_type=MESH)
     raw = [pltpu.make_async_copy(src, dst, raw_sem.at[i]) for i, (src, dst) in enumerate((
         (gg, wide_raw.at[0]), (gu, wide_raw.at[1]), (gq, q_raw), (gk, k_raw), (gv, v_raw), (gn, n_raw), (gqk, qk_raw)))]
     for copy in raw:
@@ -202,9 +205,6 @@
         start += tiles
     for f in PAIR:
         load_own(f, small=False)
-    barrier = pltpu.get_barrier_semaphore()
-    for j in OTHERS:
-        pl.semaphore_signal(barrier, inc=1, device_id=(lax.rem(me + j, DEVS),), device_id_type=MESH)
     pl.semaphore_wait(barrier, DEVS - 1)
     for f in PAIR:
         send_first(f, small=False)
@@ -412,21 +412,23 @@
         first = ag_start(owner) + k * AG_TILES
         ag_sizes(owner, k, lambda size: run(vout.at[pl.ds(first, size)], size))
 
-    def ag_link(k, mask, link):
+    def ag_link(k, mask, link, start=True):
         dev = flip(me, ORDERS[k][link])
         slot = mask + (1 << link)
 
         def copy(dst, size):
             return remote(dst, dst, ag_send.at[k, slot], ag_recv.at[k, slot], dev)
 
-        ag_each(k, mask, lambda dst, size: copy(dst, size).start())
+        if start:
+            ag_each(k, mask, lambda dst, size: copy(dst, size).start())
         pending.append(lambda: ag_each(k, mask, lambda dst, size: copy(dst, size).wait_send()))
 
-    def ag_across(k, mask):
+    def ag_across(k, mask, start=True):
         def copy(dst, size):
             return remote(dst, dst, d2d_send.at[k, mask], d2d_recv.at[k, mask], partner)
 
-        ag_each(k, mask, lambda dst, size: copy(dst, size).start())
+        if start:
+            ag_each(k, mask, lambda dst, size: copy(dst, size).start())
         pending.append(lambda: ag_each(k, mask, lambda dst, size: copy(dst, size).wait_send()))
 
     def ag_arrived(k, mask):
@@ -434,32 +436,45 @@
             dst, dst, ag_send.at[k, mask], ag_recv.at[k, mask], partner).wait_recv())
 
     pending = []
-    bounds = ((0, 52), (52, 103), (103, 153))
     base = LEAD + TILE_ROWS * ag_start(me) - SHARD_ROWS * me
-    for k in THIRDS:
-        lax.fori_loop(bounds[k][0], bounds[k][1], adam_block, 0, unroll=1)
+
+    def own_part(k, skip, count, blocks):
+        lax.fori_loop(*blocks, adam_block, 0)
         if k == 2:
             adam_rows(6120, 24)
             adam_rows(6144, 5)
-            at = pl.ds(LEAD + SHARD_ROWS, 40)
-            _, _, p = adam(grad[at, :], ext[0], ext[1], ext[2], SHARD_ROWS * (me + 1), 40)
+            at = pl.ds(LEAD + SHARD_ROWS, TILE_ROWS)
+            _, _, p = adam(grad[at, :], ext[0], ext[1], ext[2], SHARD_ROWS * (me + 1), TILE_ROWS)
             grad[at, :] = p
-
         first = ag_start(me) + k * AG_TILES
 
-        def pack(t, _, k=k, first=first):
+        def pack(t, _):
             put_tile(vout, first + t, grad, base + TILE_ROWS * (k * AG_TILES + t), COLS)
             return 0
 
-        count = ag_start(me + 1) - first if k == 2 else AG_TILES
-        lax.fori_loop(0, count, pack, 0)
-        ag_link(k, 0, 0)
-    for k in THIRDS:
-        ag_link(k, 0, 1)
-    for k in THIRDS:
-        ag_link(k, 0, 2)
-    for k in THIRDS:
-        ag_across(k, 0)
+        lax.fori_loop(skip, skip + (ag_start(me + 1) - first if k == 2 else count), pack, 0)
+
+        def send(size):
+            part = vout.at[pl.ds(first + skip, size)]
+            for link in THIRDS:
+                slot = 1 << link
+                remote(part, part, ag_send.at[k, slot], ag_recv.at[k, slot], flip(me, ORDERS[k][link])).start()
+            remote(part, part, d2d_send.at[k, 0], d2d_recv.at[k, 0], partner).start()
+
+        if k == 2:
+            ag_sizes(me, k, send)
+        else:
+            send(count)
+
+    own_part(0, 0, 13, (0, 14))
+    own_part(0, 13, 13, (14, 27))
+    own_part(0, 26, 25, (27, 52))
+    own_part(1, 0, AG_TILES, (52, 103))
+    own_part(2, 0, None, (103, 153))
+    for k in THIRDS:
+        for link in THIRDS:
+            ag_link(k, 0, link, start=False)
+        ag_across(k, 0, start=False)
     for k in THIRDS:
         ag_arrived(k, 1)
         ag_link(k, 1, 1)

time: 277 us -> 272 us (0.982)
  Pallas kernels: 276 us -> 271 us
    pallas_call x1, Pallas kernels: 265 us -> 260 us  [local_update(): pl.pallas_call(kernel, out_shape=[pltpu.VMEM((SHARD_ROWS, LANES), f32)] *...]
where the time goes in v3:
time: 272 us
  Pallas kernels  271 us (100%)
    pallas_call x1, Pallas kernels, local_update(): pl.pallas_call(kernel, out_shape=[pltpu.VMEM((SHARD_ROWS, LANES), f32)] *...  260 us
    pallas_call x1, Pallas kernels, local_update(): pl.pallas_call(flush, out_shape=[jax.ShapeDtypeStruct((EMBED_TILES, 8, WI...  11.4 us

profile of v3, /device:TPU:0, one launch (start us, length us, event | category | flops | bytes accessed | tf_op | source)
XLA Modules:
  0.0 271.6 jit_solution(15009090981091103312)
XLA Ops:
  0.7 259.6 %shard_map.237 = (f32[6149,128]{1,0:T(8,128)S(1)}, f32[6149,128]{1,0:T(8,128)S(1)}, f32[6149,128]{1,0:T(8,128)S(1)}, bf16[2496,8,640]{2,1,0:T(8,128)(2,1)S(1)}, bf16[463,8,640]{2,1,0:T(8,128)(2,1)}) custom-call(bf16[2048,8,640]{2,1,0:T(8,128)(2,1)} %bitcast.42, bf16[48,8,640]{2,1,0:T(8,128)(2,1)} %bitcast.49, bf16[12,8,640]{2,1,0:T(8,128)(2,1)} %bitcast.51, ...), custom_call_target="tpu_custom_call" | custom-call | tf_op jit(solution)/shard_map/pallas_call | solution.py:569
  260.2 11.4 %shard_map.238 = (bf16[2048,8,640]{2,1,0:T(8,128)(2,1)}, bf16[48,8,640]{2,1,0:T(8,128)(2,1)}, bf16[12,8,640]{2,1,0:T(8,128)(2,1)}, bf16[12,8,640]{2,1,0:T(8,128)...) custom-call(f32[6149,128]{1,0:T(8,128)S(1)} %get-tuple-element.30.mo, ...), custom_call_target="tpu_custom_call" | custom-call | tf_op jit(solution)/shard_map/pallas_call | solution.py:599

commit v4 on v3

--- a/solution.py
+++ b/solution.py
@@ -139,8 +139,8 @@
         dst[pl.ds(layer * width // 8, width // 8)] = block.reshape(width // 8, 8, WIDTH).astype(jnp.bfloat16)
 
 
-def kernel(emb, gq, gk, gv, go, gg, gu, gd, gn, gqk, m_in, v_in, p_in, hyp, mom, vel, par, vout, tail,
-           s1, r2, r3, ext, nsend, nrecv, wide_raw, q_raw, k_raw, v_raw, n_raw, qk_raw, n_tiles,
+def kernel(emb, gq, gk, gv, go, gg, gu, gd, gn, gqk, m_in, v_in, p_in, hyp_in, mom, vel, par, vout, tail,
+           s1, r2, r3, ext, hyp, nsend, nrecv, wide_raw, q_raw, k_raw, v_raw, n_raw, qk_raw, n_tiles,
            raw_sem, relay_sem, tail_sem,
            own_sem, r1_send, r1_recv, r2_send, r2_recv, r3_send, r3_recv, st_sem,
            ext_send, ext_recv, n_send, n_recv, ag_send, ag_recv, d2d_send, d2d_recv):
@@ -169,7 +169,7 @@
         return flip_mask(dev, ORDERS[k], (0 if f >= 2 else 2) + (4 if f % 2 == 0 else 0))
 
     state = [pltpu.make_async_copy(src, dst, st_sem.at[i])
-             for i, (src, dst) in enumerate(((m_in, mom), (v_in, vel), (p_in, par)))]
+             for i, (src, dst) in enumerate(((m_in, mom), (v_in, vel), (p_in, par), (hyp_in, hyp)))]
 
     def load_own(f, embed=True, small=True):
         for k in THIRDS:
@@ -187,8 +187,10 @@
                     embed, small)
 
     barrier = pltpu.get_barrier_semaphore()
-    for j in OTHERS:
-        pl.semaphore_signal(barrier, inc=1, device_id=(lax.rem(me + j, DEVS),), device_id_type=MESH)
+    near = [flip(me, order[0]) for order in ORDERS]
+    near += [flip(dev, 1) for dev in near] + [partner]
+    for dev in near:
+        pl.semaphore_signal(barrier, inc=1, device_id=(dev,), device_id_type=MESH)
     raw = [pltpu.make_async_copy(src, dst, raw_sem.at[i]) for i, (src, dst) in enumerate((
         (gg, wide_raw.at[0]), (gu, wide_raw.at[1]), (gq, q_raw), (gk, k_raw), (gv, v_raw), (gn, n_raw), (gqk, qk_raw)))]
     for copy in raw:
@@ -205,8 +207,8 @@
         start += tiles
     for f in PAIR:
         load_own(f, small=False)
-    pl.semaphore_wait(barrier, DEVS - 1)
-    for f in PAIR:
+    pl.semaphore_wait(barrier, len(near))
+    for f in THIRDS:
         send_first(f, small=False)
 
     for copy, onward in relayed:
@@ -251,17 +253,12 @@
     to_tail(n_tiles.at[pl.ds(3, 1)], "qk")
     for copy in onwards:
         copy.wait()
-    for f in PAIR:
-        send_first(f, embed=False)
-        load_own(f, embed=False)
-    for f in range(2, 4):
-        send_first(f)
-        load_own(f)
+    for f in range(4):
+        send_first(f, embed=f == 3)
+        load_own(f, embed=f > 1)
     before = lax.rem(me + DEVS - 1, DEVS)
     ext_copies = [remote(src.at[pl.ds(0, TILE_ROWS)], ext.at[i], ext_send.at[i], ext_recv.at[i], before)
                   for i, src in enumerate((m_in, v_in, p_in))]
-    for copy in ext_copies:
-        copy.start()
     for copy in state:
         copy.start()
 
@@ -324,6 +321,8 @@
             return 0
 
         lax.fori_loop(0, RS_TILES, finish, 0, unroll=2)
+    for copy in ext_copies:
+        copy.start()
 
     def squares(i, acc):
         part = grad[pl.ds(pl.multiple_of(LEAD + i * 40, 8), 40), :]
@@ -343,6 +342,9 @@
     for j in OTHERS:
         n_copy(j).start()
 
+    for copy in state:
+        copy.wait()
+
     def full(value):
         return jnp.full((8, LANES), value, jnp.float32)
 
@@ -350,8 +352,6 @@
     rest_one, rest_two = 1.0 - beta_one, 1.0 - beta_two
     hat_one = 1.0 / (1.0 - lax.integer_pow(beta_one, ADAM_STEP))
     hat_two = 1.0 / (1.0 - lax.integer_pow(beta_two, ADAM_STEP))
-    for copy in state:
-        copy.wait()
     for copy in ext_copies:
         copy.wait_recv()
 
@@ -571,13 +571,14 @@
             out_shape=[pltpu.VMEM((SHARD_ROWS, LANES), f32)] * 3
             + [pltpu.VMEM((OUT_TILES, 8, WIDTH), bf16)]
             + [pltpu.HBM((TAIL_TILES, 8, WIDTH), bf16)],
-            in_specs=[any_spec] * 13 + [pl.BlockSpec(memory_space=pltpu.SMEM)],
+            in_specs=[any_spec] * 14,
             out_specs=[vmem_spec] * 4 + [any_spec],
             scratch_shapes=[
                 pltpu.VMEM((3 * 4 * PIECE_ROWS, LANES), f32),
                 pltpu.VMEM((3, 2, PIECE_ROWS, LANES), f32),
                 pltpu.VMEM((3, PIECE_ROWS, LANES), f32),
                 pltpu.VMEM((3, TILE_ROWS, LANES), f32),
+                pltpu.SMEM((5,), f32),
                 pltpu.VMEM((8, LANES), f32),
                 pltpu.VMEM((DEVS, 8, LANES), f32),
                 pltpu.VMEM((2, 3840, LANES), bf16),
@@ -589,7 +590,7 @@
                 pltpu.VMEM((4, 8, WIDTH), bf16),
                 dma((7,)), dma((3,)), dma((3 + len(SMALL),)),
                 dma((3, 4)), dma((3, 3, 4)), dma((3, 3, 4)), dma((3, 2)), dma((3, 2)), dma((3,)), dma((3,)),
-                dma((3,)), dma((3,)), dma((3,)), dma((DEVS,)), dma((DEVS,)),
+                dma((4,)), dma((3,)), dma((3,)), dma((DEVS,)), dma((DEVS,)),
                 dma((3, 8)), dma((3, 8)), dma((3, 8)), dma((3, 8)),
             ],
             compiler_params=pltpu.CompilerParams(

time: 272 us -> 271 us (level)
  no operation moved by 1% of the time
where the time goes in v4:
time: 271 us
  Pallas kernels  270 us (100%)
    pallas_call x1, Pallas kernels, local_update(): pl.pallas_call(kernel, out_shape=[pltpu.VMEM((SHARD_ROWS, LANES), f32)] *...  259 us
    pallas_call x1, Pallas kernels, local_update(): pl.pallas_call(flush, out_shape=[jax.ShapeDtypeStruct((EMBED_TILES, 8, WI...  11.4 us

profile of v4, /device:TPU:0, one launch (start us, length us, event | category | flops | bytes accessed | tf_op | source)
XLA Modules:
  0.0 270.6 jit_solution(8554144216050191959)
XLA Ops:
  0.7 258.6 %shard_map.237 = (f32[6149,128]{1,0:T(8,128)S(1)}, f32[6149,128]{1,0:T(8,128)S(1)}, f32[6149,128]{1,0:T(8,128)S(1)}, bf16[2496,8,640]{2,1,0:T(8,128)(2,1)S(1)}, bf16[463,8,640]{2,1,0:T(8,128)(2,1)}) custom-call(bf16[2048,8,640]{2,1,0:T(8,128)(2,1)} %bitcast.42, bf16[48,8,640]{2,1,0:T(8,128)(2,1)} %bitcast.49, bf16[12,8,640]{2,1,0:T(8,128)(2,1)} %bitcast.51, ...), custom_call_target="tpu_custom_call" | custom-call | tf_op jit(solution)/shard_map/pallas_call | solution.py:569
  259.2 11.4 %shard_map.238 = (bf16[2048,8,640]{2,1,0:T(8,128)(2,1)}, bf16[48,8,640]{2,1,0:T(8,128)(2,1)}, bf16[12,8,640]{2,1,0:T(8,128)(2,1)}, bf16[12,8,640]{2,1,0:T(8,128)...) custom-call(f32[6149,128]{1,0:T(8,128)S(1)} %get-tuple-element.30.mo, ...), custom_call_target="tpu_custom_call" | custom-call | tf_op jit(solution)/shard_map/pallas_call | solution.py:600

commit v5 on v4

--- a/solution.py
+++ b/solution.py
@@ -29,6 +29,9 @@
 RS_TILES = 52
 TAIL_TILES = (SHARD_ROWS * 15) // TILE_ROWS + 3 * RS_TILES - TAIL_START
 AG_TILES = 51
+PART_TILES = 13
+LAST_PART = 3
+FLUSH_PARTS = 16
 LEAD = 40
 G_ROWS = LEAD + 3 * RS_TILES * TILE_ROWS
 ORDERS = ((2, 4, 8), (4, 8, 2), (8, 2, 4))
@@ -63,6 +66,8 @@
 OUT_TILES = 48 * RS_TILES
 SPARE = 42 * RS_TILES
 PIECE_ROWS = RS_TILES * TILE_ROWS
+HALF_TILES = RS_TILES // 2
+HALF_ROWS = PIECE_ROWS // 2
 
 
 def slot_tiles(slot, k, f):
@@ -143,7 +148,7 @@
            s1, r2, r3, ext, hyp, nsend, nrecv, wide_raw, q_raw, k_raw, v_raw, n_raw, qk_raw, n_tiles,
            raw_sem, relay_sem, tail_sem,
            own_sem, r1_send, r1_recv, r2_send, r2_recv, r3_send, r3_recv, st_sem,
-           ext_send, ext_recv, n_send, n_recv, ag_send, ag_recv, d2d_send, d2d_recv):
+           ext_send, ext_recv, n_send, n_recv, ag_send, ag_recv, d2d_send, d2d_recv, last_recv):
     grad = s1.at[pl.ds(0, G_ROWS)]
     me = lax.axis_index("dp")
     partner = flip(me, 1)
@@ -269,8 +274,10 @@
     def r2_copy(k, f):
         return remote(s1.at[sum_rows(k, f)], r2.at[k, f], r2_send.at[k, f], r2_recv.at[k, f], flip(me, ORDERS[k][1]))
 
-    def r3_copy(k):
-        return remote(s1.at[sum_rows(k, 2)], r3.at[k], r3_send.at[k], r3_recv.at[k], flip(me, ORDERS[k][2]))
+    def r3_copy(k, half):
+        src = pl.ds(sum_rows(k, 2).start + half * HALF_ROWS, HALF_ROWS)
+        dst = pl.ds(half * HALF_ROWS, HALF_ROWS)
+        return remote(s1.at[src], r3.at[k, dst], r3_send.at[k, half], r3_recv.at[k, half], flip(me, ORDERS[k][2]))
 
     for f in range(4):
         for k in THIRDS:
@@ -300,47 +307,54 @@
                 s1[at, :] = s1[at, :] + r2[k, f, pl.ds(row, TILE_ROWS), :]
                 return 0
 
-            lax.fori_loop(0, RS_TILES, add_two, 0, unroll=2)
-            if f == 0:
-                r3_copy(k).start()
+            for half in PAIR:
+                lax.fori_loop(half * HALF_TILES, (half + 1) * HALF_TILES, add_two, 0, unroll=2)
+                if f == 0:
+                    r3_copy(k, half).start()
 
     shift = LEAD - (SHARD_ROWS * me - TILE_ROWS * rs_start(me))
     for k in THIRDS:
         for f in PAIR:
             r2_copy(k, f).wait_send()
-    for k in THIRDS:
-        r3_copy(k).wait_recv()
-
-        def finish(t, _, k=k):
-            row = pl.multiple_of(TILE_ROWS * t, 8)
-            at = pl.ds(pl.multiple_of(sum_rows(k, 3).start + TILE_ROWS * t, 8), TILE_ROWS)
-            total = (s1[at, :] + r3[k, pl.ds(row, TILE_ROWS), :]) * (1.0 / DEVS)
-            row = shift + TILE_ROWS * (k * RS_TILES + t)
-            for j in range(COLS):
-                grad[pl.ds(row + j, 8, stride=COLS), :] = total[8 * j:8 * (j + 1), :]
-            return 0
-
-        lax.fori_loop(0, RS_TILES, finish, 0, unroll=2)
+    def squares(i, acc):
+        part = grad[pl.ds(pl.multiple_of(i * TILE_ROWS, 8), TILE_ROWS), :]
+        return acc + part * part
+
+    def finish(k, t, carry):
+        row = pl.multiple_of(TILE_ROWS * t, 8)
+        at = pl.ds(pl.multiple_of(sum_rows(k, 3).start + TILE_ROWS * t, 8), TILE_ROWS)
+        total = (s1[at, :] + r3[k, pl.ds(row, TILE_ROWS), :]) * (1.0 / DEVS)
+        row = shift + TILE_ROWS * (k * RS_TILES + t)
+        for j in range(COLS):
+            grad[pl.ds(row + j, 8, stride=COLS), :] = total[8 * j:8 * (j + 1), :]
+        return carry
+
+    acc = jnp.zeros((TILE_ROWS, LANES), jnp.float32)
+    end = (LEAD + SHARD_ROWS) // TILE_ROWS
+    for half in PAIR:
+        for k in THIRDS:
+            r3_copy(k, half).wait_recv()
+            lax.fori_loop(half * HALF_TILES, (half + 1) * HALF_TILES, functools.partial(finish, k), 0, unroll=2)
+        for k in THIRDS:
+            first = k * RS_TILES + 1
+            middle = first + HALF_TILES - 1
+            blocks = (middle, min(first + RS_TILES, end)) if half else (first, middle)
+            acc = lax.fori_loop(*blocks, squares, acc, unroll=3)
     for copy in ext_copies:
         copy.start()
-
-    def squares(i, acc):
-        part = grad[pl.ds(pl.multiple_of(LEAD + i * 40, 8), 40), :]
-        return acc + part * part
-
-    acc = lax.fori_loop(0, 153, squares, jnp.zeros((40, LANES), jnp.float32), unroll=3)
     nsend[...] = acc[0:8] + acc[8:16] + acc[16:24] + acc[24:32] + acc[32:40]
-    for row in (6120, 6128, 6136):
-        part = grad[pl.ds(LEAD + row, 8), :]
-        nsend[...] = nsend[...] + part * part
-    part = grad[pl.ds(LEAD + 6144, 5), :]
-    nsend[0:5, :] = nsend[0:5, :] + part * part
-
-    def n_copy(j):
-        return remote(nsend, nrecv.at[me], n_send.at[j], n_recv.at[me], lax.rem(me + j, DEVS))
-
-    for j in OTHERS:
-        n_copy(j).start()
+    start = end * TILE_ROWS
+    for row, rows in ((start, 8), (start + 8, 8), (start + 16, 8), (start + 24, 5)):
+        part = grad[pl.ds(row, rows), :]
+        nsend[0:rows, :] = nsend[0:rows, :] + part * part
+
+    others = [flip_mask(me, (1, 2, 4, 8), mask) for mask in sorted(OTHERS, key=lambda mask: -(mask // 2).bit_count())]
+
+    def n_copy(i, source):
+        return remote(nsend, nrecv.at[source], n_send.at[i], n_recv.at[source], others[i])
+
+    for i in range(len(others)):
+        n_copy(i, me).start()
 
     for copy in state:
         copy.wait()
@@ -355,10 +369,9 @@
     for copy in ext_copies:
         copy.wait_recv()
 
-    for j in OTHERS:
-        n_copy(j).wait_send()
-        source = lax.rem(me + DEVS - j, DEVS)
-        remote(nsend, nrecv.at[source], n_send.at[j], n_recv.at[source], partner).wait_recv()
+    for i, dev in enumerate(others):
+        n_copy(i, me).wait_send()
+        n_copy(i, dev).wait_recv()
     nrecv[me] = nsend[...]
     total = nrecv[0]
     for j in OTHERS:
@@ -422,6 +435,20 @@
         if start:
             ag_each(k, mask, lambda dst, size: copy(dst, size).start())
         pending.append(lambda: ag_each(k, mask, lambda dst, size: copy(dst, size).wait_send()))
+
+    def ag_part(k, mask, i, run):
+        owner = flip_mask(me, ORDERS[k], mask)
+        first = ag_start(owner) + k * AG_TILES + i * PART_TILES
+        if i < LAST_PART:
+            run(vout.at[pl.ds(first, PART_TILES)])
+        else:
+            ag_sizes(owner, k, lambda size: run(vout.at[pl.ds(first, size - LAST_PART * PART_TILES)]))
+
+    def last_copy(k, i, part):
+        return remote(part, part, ag_send.at[k, 7], last_recv.at[k, i], flip(me, ORDERS[k][2]))
+
+    def across_copy(k, part):
+        return remote(part, part, d2d_send.at[k, 7], d2d_recv.at[k, 7], partner)
 
     def ag_across(k, mask, start=True):
         def copy(dst, size):
@@ -466,9 +493,9 @@
         else:
             send(count)
 
-    own_part(0, 0, 13, (0, 14))
-    own_part(0, 13, 13, (14, 27))
-    own_part(0, 26, 25, (27, 52))
+    own_part(0, 0, 7, (0, 8))
+    own_part(0, 7, 14, (8, 22))
+    own_part(0, 21, 30, (22, 52))
     own_part(1, 0, AG_TILES, (52, 103))
     own_part(2, 0, None, (103, 153))
     for k in THIRDS:
@@ -490,12 +517,20 @@
         ag_across(k, 4)
     for k in THIRDS:
         ag_arrived(k, 3)
-        ag_link(k, 3, 2)
+        for i in range(LAST_PART + 1):
+            ag_part(k, 3, i, lambda part, k=k, i=i: last_copy(k, i, part).start())
+        ag_link(k, 3, 2, start=False)
         ag_across(k, 3)
-    for mask in (5, 6, 7):
+    for mask in (5, 6):
         for k in THIRDS:
             ag_arrived(k, mask)
             ag_across(k, mask)
+    for i in range(LAST_PART + 1):
+        for k in THIRDS:
+            ag_part(k, 7, i, lambda part, k=k, i=i: last_copy(k, i, part).wait_recv())
+            ag_part(k, 7, i, lambda part, k=k, i=i: across_copy(k, part).start())
+    for k in THIRDS:
+        ag_across(k, 7, start=False)
     for mask in range(8):
         for k in THIRDS:
             ag_each(k, mask, lambda dst, size, k=k, mask=mask: remote(
@@ -509,7 +544,8 @@
             for slot in THIRDS:
                 r1_copy(slot, k, f).wait_send()
     for k in THIRDS:
-        r3_copy(k).wait_send()
+        for half in PAIR:
+            r3_copy(k, half).wait_send()
 
 
 def flush(mom, vel, par, vout, embed, oq, ok, ov, oo, og, ou, od, on, oqk, m_out, v_out, p_out,
@@ -521,8 +557,8 @@
         copy.start()
         copies.append(copy)
 
-    for i in range(4):
-        part = pl.ds(i * EMBED_TILES // 4, EMBED_TILES // 4)
+    for i in range(FLUSH_PARTS):
+        part = pl.ds(i * (EMBED_TILES // FLUSH_PARTS), EMBED_TILES // FLUSH_PARTS)
         send(vout.at[part], embed.at[part])
     for src, dst in ((mom, m_out), (vel, v_out), (par, p_out)):
         send(src, dst)
@@ -589,9 +625,9 @@
                 pltpu.VMEM(shapes[9], bf16),
                 pltpu.VMEM((4, 8, WIDTH), bf16),
                 dma((7,)), dma((3,)), dma((3 + len(SMALL),)),
-                dma((3, 4)), dma((3, 3, 4)), dma((3, 3, 4)), dma((3, 2)), dma((3, 2)), dma((3,)), dma((3,)),
+                dma((3, 4)), dma((3, 3, 4)), dma((3, 3, 4)), dma((3, 2)), dma((3, 2)), dma((3, 2)), dma((3, 2)),
                 dma((4,)), dma((3,)), dma((3,)), dma((DEVS,)), dma((DEVS,)),
-                dma((3, 8)), dma((3, 8)), dma((3, 8)), dma((3, 8)),
+                dma((3, 8)), dma((3, 8)), dma((3, 8)), dma((3, 8)), dma((3, LAST_PART + 1)),
             ],
             compiler_params=pltpu.CompilerParams(
                 collective_id=0, has_side_effects=True, vmem_limit_bytes=26_500_000),
@@ -611,7 +647,7 @@
                 pltpu.VMEM((12, 8, WIDTH), bf16),
                 pltpu.VMEM(shapes[8], bf16),
                 pltpu.VMEM(shapes[9], bf16),
-                dma((20,)),
+                dma((FLUSH_PARTS + 16,)),
             ],
             compiler_params=pltpu.CompilerParams(has_side_effects=True, vmem_limit_bytes=5_200_000),
         )(*kept)

time: 271 us -> 269 us (level)
  no operation moved by 1% of the time
where the time goes in v5:
time: 269 us
  Pallas kernels  269 us (100%)
    pallas_call x1, Pallas kernels, local_update(): pl.pallas_call(kernel, out_shape=[pltpu.VMEM((SHARD_ROWS, LANES), f32)] *...  257 us
    pallas_call x1, Pallas kernels, local_update(): pl.pallas_call(flush, out_shape=[jax.ShapeDtypeStruct((EMBED_TILES, 8, WI...  11.5 us

profile of v5, /device:TPU:0, one launch (start us, length us, event | category | flops | bytes accessed | tf_op | source)
XLA Modules:
  0.0 269.2 jit_solution(14531437159217881795)
XLA Ops:
  0.7 257.1 %shard_map.237 = (f32[6149,128]{1,0:T(8,128)S(1)}, f32[6149,128]{1,0:T(8,128)S(1)}, f32[6149,128]{1,0:T(8,128)S(1)}, bf16[2496,8,640]{2,1,0:T(8,128)(2,1)S(1)}, bf16[463,8,640]{2,1,0:T(8,128)(2,1)}) custom-call(bf16[2048,8,640]{2,1,0:T(8,128)(2,1)} %bitcast.42, bf16[48,8,640]{2,1,0:T(8,128)(2,1)} %bitcast.49, bf16[12,8,640]{2,1,0:T(8,128)(2,1)} %bitcast.51, ...), custom_call_target="tpu_custom_call" | custom-call | tf_op jit(solution)/shard_map/pallas_call | solution.py:605
  257.7 11.5 %shard_map.238 = (bf16[2048,8,640]{2,1,0:T(8,128)(2,1)}, bf16[48,8,640]{2,1,0:T(8,128)(2,1)}, bf16[12,8,640]{2,1,0:T(8,128)(2,1)}, bf16[12,8,640]{2,1,0:T(8,128)...) custom-call(f32[6149,128]{1,0:T(8,128)S(1)} %get-tuple-element.30.mo, ...), custom_call_target="tpu_custom_call" | custom-call | tf_op jit(solution)/shard_map/pallas_call | solution.py:636

commit v6 on v5

--- a/solution.py
+++ b/solution.py
@@ -29,9 +29,9 @@
 RS_TILES = 52
 TAIL_TILES = (SHARD_ROWS * 15) // TILE_ROWS + 3 * RS_TILES - TAIL_START
 AG_TILES = 51
-PART_TILES = 13
+PART_TILES = 15
 LAST_PART = 3
-FLUSH_PARTS = 16
+FLUSH_PARTS = 4
 LEAD = 40
 G_ROWS = LEAD + 3 * RS_TILES * TILE_ROWS
 ORDERS = ((2, 4, 8), (4, 8, 2), (8, 2, 4))
@@ -145,10 +145,10 @@
 
 
 def kernel(emb, gq, gk, gv, go, gg, gu, gd, gn, gqk, m_in, v_in, p_in, hyp_in, mom, vel, par, vout, tail,
-           s1, r2, r3, ext, hyp, nsend, nrecv, wide_raw, q_raw, k_raw, v_raw, n_raw, qk_raw, n_tiles,
+           s1, r2, r3, ext, hyp, ahead, nsend, nrecv, wide_raw, q_raw, k_raw, v_raw, n_raw, qk_raw, n_tiles,
            raw_sem, relay_sem, tail_sem,
            own_sem, r1_send, r1_recv, r2_send, r2_recv, r3_send, r3_recv, st_sem,
-           ext_send, ext_recv, n_send, n_recv, ag_send, ag_recv, d2d_send, d2d_recv, last_recv):
+           ext_send, ext_recv, n_send, n_recv, ag_send, ag_recv, d2d_send, d2d_recv, last_recv, ahead_sem):
     grad = s1.at[pl.ds(0, G_ROWS)]
     me = lax.axis_index("dp")
     partner = flip(me, 1)
@@ -157,18 +157,18 @@
         return pltpu.make_async_remote_copy(
             src_ref=src, dst_ref=dst, send_sem=ssem, recv_sem=rsem, device_id=(dev,), device_id_type=MESH)
 
-    def from_shard(owner, k, make, embed=True, small=True):
+    def from_shard(owner, k, make, embed=True, small=True, act=lambda copy: copy.start()):
         first = rs_start(owner) + k * RS_TILES
 
         if embed:
             @pl.when(owner < FIRST_TAIL)
             def _():
-                make(emb.at[pl.ds(first, RS_TILES)]).start()
+                act(make(emb.at[pl.ds(first, RS_TILES)]))
 
         if small:
             @pl.when(owner >= FIRST_TAIL)
             def _():
-                make(tail.at[pl.ds(first - TAIL_START, RS_TILES)]).start()
+                act(make(tail.at[pl.ds(first - TAIL_START, RS_TILES)]))
 
     def rs_owner(dev, k, f):
         return flip_mask(dev, ORDERS[k], (0 if f >= 2 else 2) + (4 if f % 2 == 0 else 0))
@@ -181,21 +181,35 @@
             from_shard(rs_owner(me, k, f), k, lambda src, k=k: pltpu.make_async_copy(
                 src, vout.at[slot_tiles(3, k, f)], own_sem.at[k, f]), embed, small)
 
+    def first_owner(slot, k, f):
+        dev = partner if slot == 2 else flip(me, ORDERS[k][0])
+        if slot == 1:
+            dev = flip(dev, 1)
+        return dev, rs_owner(dev, k, f)
+
     def send_first(f, embed=True, small=True):
-        for k in THIRDS:
-            for slot in THIRDS:
-                dev = partner if slot == 2 else flip(me, ORDERS[k][0])
-                if slot == 1:
-                    dev = flip(dev, 1)
-                from_shard(rs_owner(dev, k, f), k, lambda src, k=k, slot=slot, dev=dev: remote(
-                    src, vout.at[slot_tiles(slot, k, f)], r1_send.at[slot, k, f], r1_recv.at[slot, k, f], dev),
-                    embed, small)
+        for slot in THIRDS:
+            for k in THIRDS:
+                dev, owner = first_owner(slot, k, f)
+
+                def make(src, k=k, slot=slot, dev=dev):
+                    src = ahead.at[k] if embed and not small and f + slot == 0 else src
+                    return remote(src, vout.at[slot_tiles(slot, k, f)], r1_send.at[slot, k, f],
+                                  r1_recv.at[slot, k, f], dev)
+
+                from_shard(owner, k, make, embed, small)
+
+    def load_ahead(act):
+        for k in THIRDS:
+            from_shard(first_owner(0, k, 0)[1], k, lambda src, k=k: pltpu.make_async_copy(
+                src, ahead.at[k], ahead_sem.at[k]), small=False, act=act)
 
     barrier = pltpu.get_barrier_semaphore()
     near = [flip(me, order[0]) for order in ORDERS]
     near += [flip(dev, 1) for dev in near] + [partner]
     for dev in near:
         pl.semaphore_signal(barrier, inc=1, device_id=(dev,), device_id_type=MESH)
+    load_ahead(lambda copy: copy.start())
     raw = [pltpu.make_async_copy(src, dst, raw_sem.at[i]) for i, (src, dst) in enumerate((
         (gg, wide_raw.at[0]), (gu, wide_raw.at[1]), (gq, q_raw), (gk, k_raw), (gv, v_raw), (gn, n_raw), (gqk, qk_raw)))]
     for copy in raw:
@@ -212,6 +226,7 @@
         start += tiles
     for f in PAIR:
         load_own(f, small=False)
+    load_ahead(lambda copy: copy.wait())
     pl.semaphore_wait(barrier, len(near))
     for f in THIRDS:
         send_first(f, small=False)
@@ -512,6 +527,15 @@
         ag_arrived(k, 2)
         ag_link(k, 2, 2)
         ag_across(k, 2)
+    for copy in ext_copies:
+        copy.wait_send()
+    for f in range(4):
+        for k in THIRDS:
+            for slot in THIRDS:
+                r1_copy(slot, k, f).wait_send()
+    for k in THIRDS:
+        for half in PAIR:
+            r3_copy(k, half).wait_send()
     for k in THIRDS:
         ag_arrived(k, 4)
         ag_across(k, 4)
@@ -519,33 +543,31 @@
         ag_arrived(k, 3)
         for i in range(LAST_PART + 1):
             ag_part(k, 3, i, lambda part, k=k, i=i: last_copy(k, i, part).start())
-        ag_link(k, 3, 2, start=False)
         ag_across(k, 3)
     for mask in (5, 6):
         for k in THIRDS:
             ag_arrived(k, mask)
             ag_across(k, mask)
+    def from_partner(masks):
+        for mask in masks:
+            for k in THIRDS:
+                ag_each(k, mask, lambda dst, size, k=k, mask=mask: remote(
+                    dst, dst, d2d_send.at[k, mask], d2d_recv.at[k, mask], partner).wait_recv(), partner)
+
+    from_partner(range(5))
+    for wait in pending:
+        wait()
+    pending.clear()
     for i in range(LAST_PART + 1):
         for k in THIRDS:
             ag_part(k, 7, i, lambda part, k=k, i=i: last_copy(k, i, part).wait_recv())
             ag_part(k, 7, i, lambda part, k=k, i=i: across_copy(k, part).start())
     for k in THIRDS:
+        ag_link(k, 3, 2, start=False)
         ag_across(k, 7, start=False)
-    for mask in range(8):
-        for k in THIRDS:
-            ag_each(k, mask, lambda dst, size, k=k, mask=mask: remote(
-                dst, dst, d2d_send.at[k, mask], d2d_recv.at[k, mask], partner).wait_recv(), partner)
+    from_partner(range(5, 8))
     for wait in pending:
         wait()
-    for copy in ext_copies:
-        copy.wait_send()
-    for f in range(4):
-        for k in THIRDS:
-            for slot in THIRDS:
-                r1_copy(slot, k, f).wait_send()
-    for k in THIRDS:
-        for half in PAIR:
-            r3_copy(k, half).wait_send()
 
 
 def flush(mom, vel, par, vout, embed, oq, ok, ov, oo, og, ou, od, on, oqk, m_out, v_out, p_out,
@@ -615,6 +637,7 @@
                 pltpu.VMEM((3, PIECE_ROWS, LANES), f32),
                 pltpu.VMEM((3, TILE_ROWS, LANES), f32),
                 pltpu.SMEM((5,), f32),
+                pltpu.VMEM((3, RS_TILES, 8, WIDTH), bf16),
                 pltpu.VMEM((8, LANES), f32),
                 pltpu.VMEM((DEVS, 8, LANES), f32),
                 pltpu.VMEM((2, 3840, LANES), bf16),
@@ -627,10 +650,10 @@
                 dma((7,)), dma((3,)), dma((3 + len(SMALL),)),
                 dma((3, 4)), dma((3, 3, 4)), dma((3, 3, 4)), dma((3, 2)), dma((3, 2)), dma((3, 2)), dma((3, 2)),
                 dma((4,)), dma((3,)), dma((3,)), dma((DEVS,)), dma((DEVS,)),
-                dma((3, 8)), dma((3, 8)), dma((3, 8)), dma((3, 8)), dma((3, LAST_PART + 1)),
+                dma((3, 8)), dma((3, 8)), dma((3, 8)), dma((3, 8)), dma((3, LAST_PART + 1)), dma((3,)),
             ],
             compiler_params=pltpu.CompilerParams(
-                collective_id=0, has_side_effects=True, vmem_limit_bytes=26_500_000),
+                collective_id=0, has_side_effects=True, vmem_limit_bytes=26_960_000),
         )(*tiled, *state, arrays[GRAD_COUNT + 3])
         kept = [pltpu.with_memory_space_constraint(arr, pltpu.VMEM) for arr in kept]
         outs = pl.pallas_call(
@@ -649,7 +672,7 @@
                 pltpu.VMEM(shapes[9], bf16),
                 dma((FLUSH_PARTS + 16,)),
             ],
-            compiler_params=pltpu.CompilerParams(has_side_effects=True, vmem_limit_bytes=5_200_000),
+            compiler_params=pltpu.CompilerParams(has_side_effects=True, vmem_limit_bytes=4_800_000),
         )(*kept)
         params = []
         for i, dims in enumerate(shapes):

time: 269 us -> 271 us (level)
  no operation moved by 1% of the time
where the time goes in v6:
time: 271 us
  Pallas kernels  270 us (100%)
    pallas_call x1, Pallas kernels, local_update(): pl.pallas_call(kernel, out_shape=[pltpu.VMEM((SHARD_ROWS, LANES), f32)] *...  259 us
    pallas_call x1, Pallas kernels, local_update(): pl.pallas_call(flush, out_shape=[jax.ShapeDtypeStruct((EMBED_TILES, 8, WI...  11.4 us

profile of v6, /device:TPU:0, one launch (start us, length us, event | category | flops | bytes accessed | tf_op | source)
XLA Modules:
  0.0 270.9 jit_solution(17787124671118221657)
XLA Ops:
  0.7 258.9 %shard_map.237 = (f32[6149,128]{1,0:T(8,128)S(1)}, f32[6149,128]{1,0:T(8,128)S(1)}, f32[6149,128]{1,0:T(8,128)S(1)}, bf16[2496,8,640]{2,1,0:T(8,128)(2,1)S(1)}, bf16[463,8,640]{2,1,0:T(8,128)(2,1)}) custom-call(bf16[2048,8,640]{2,1,0:T(8,128)(2,1)} %bitcast.42, bf16[48,8,640]{2,1,0:T(8,128)(2,1)} %bitcast.49, bf16[12,8,640]{2,1,0:T(8,128)(2,1)} %bitcast.51, ...), custom_call_target="tpu_custom_call" | custom-call | tf_op jit(solution)/shard_map/pallas_call | solution.py:627
  259.6 11.4 %shard_map.238 = (bf16[2048,8,640]{2,1,0:T(8,128)(2,1)}, bf16[48,8,640]{2,1,0:T(8,128)(2,1)}, bf16[12,8,640]{2,1,0:T(8,128)(2,1)}, bf16[12,8,640]{2,1,0:T(8,128)...) custom-call(f32[6149,128]{1,0:T(8,128)S(1)} %get-tuple-element.30.mo, ...), custom_call_target="tpu_custom_call" | custom-call | tf_op jit(solution)/shard_map/pallas_call | solution.py:659

commit v7 on v6

--- a/solution.py
+++ b/solution.py
@@ -29,7 +29,7 @@
 RS_TILES = 52
 TAIL_TILES = (SHARD_ROWS * 15) // TILE_ROWS + 3 * RS_TILES - TAIL_START
 AG_TILES = 51
-PART_TILES = 15
+PART_TILES = 16
 LAST_PART = 3
 FLUSH_PARTS = 4
 LEAD = 40
@@ -39,6 +39,10 @@
 
 def flip(dev, stride):
     return dev + stride - 2 * stride * lax.rem(dev // stride, 2)
+
+
+def rs_tiles(k):
+    return RS_TILES - k // 2
 
 
 def rs_start(dev):
@@ -66,17 +70,17 @@
 OUT_TILES = 48 * RS_TILES
 SPARE = 42 * RS_TILES
 PIECE_ROWS = RS_TILES * TILE_ROWS
-HALF_TILES = RS_TILES // 2
-HALF_ROWS = PIECE_ROWS // 2
+QUARTERS = range(4)
+QUARTER = RS_TILES // 4
 
 
 def slot_tiles(slot, k, f):
     index = 36 + f * 3 + k if slot == 3 else (slot * 3 + k) * 4 + f
-    return pl.ds(index * RS_TILES, RS_TILES)
+    return pl.ds(index * RS_TILES, rs_tiles(k))
 
 
 def sum_rows(k, f):
-    return pl.ds((f * 3 + k) * PIECE_ROWS, PIECE_ROWS)
+    return pl.ds((f * 3 + k) * PIECE_ROWS, rs_tiles(k) * TILE_ROWS)
 
 
 def put_tile(dst, tile, rows, first, stride):
@@ -145,10 +149,10 @@
 
 
 def kernel(emb, gq, gk, gv, go, gg, gu, gd, gn, gqk, m_in, v_in, p_in, hyp_in, mom, vel, par, vout, tail,
-           s1, r2, r3, ext, hyp, ahead, nsend, nrecv, wide_raw, q_raw, k_raw, v_raw, n_raw, qk_raw, n_tiles,
+           s1, r2, r3, ext, hyp, nsend, nrecv, wide_raw, q_raw, k_raw, v_raw, n_raw, qk_raw, n_tiles,
            raw_sem, relay_sem, tail_sem,
            own_sem, r1_send, r1_recv, r2_send, r2_recv, r3_send, r3_recv, st_sem,
-           ext_send, ext_recv, n_send, n_recv, ag_send, ag_recv, d2d_send, d2d_recv, last_recv, ahead_sem):
+           ext_send, ext_recv, n_send, n_recv, ag_send, ag_recv, d2d_send, d2d_recv, last_recv):
     grad = s1.at[pl.ds(0, G_ROWS)]
     me = lax.axis_index("dp")
     partner = flip(me, 1)
@@ -157,18 +161,18 @@
         return pltpu.make_async_remote_copy(
             src_ref=src, dst_ref=dst, send_sem=ssem, recv_sem=rsem, device_id=(dev,), device_id_type=MESH)
 
-    def from_shard(owner, k, make, embed=True, small=True, act=lambda copy: copy.start()):
+    def from_shard(owner, k, make, embed=True, small=True):
         first = rs_start(owner) + k * RS_TILES
 
         if embed:
             @pl.when(owner < FIRST_TAIL)
             def _():
-                act(make(emb.at[pl.ds(first, RS_TILES)]))
+                make(emb.at[pl.ds(first, rs_tiles(k))]).start()
 
         if small:
             @pl.when(owner >= FIRST_TAIL)
             def _():
-                act(make(tail.at[pl.ds(first - TAIL_START, RS_TILES)]))
+                make(tail.at[pl.ds(first - TAIL_START, rs_tiles(k))]).start()
 
     def rs_owner(dev, k, f):
         return flip_mask(dev, ORDERS[k], (0 if f >= 2 else 2) + (4 if f % 2 == 0 else 0))
@@ -193,23 +197,16 @@
                 dev, owner = first_owner(slot, k, f)
 
                 def make(src, k=k, slot=slot, dev=dev):
-                    src = ahead.at[k] if embed and not small and f + slot == 0 else src
                     return remote(src, vout.at[slot_tiles(slot, k, f)], r1_send.at[slot, k, f],
                                   r1_recv.at[slot, k, f], dev)
 
                 from_shard(owner, k, make, embed, small)
-
-    def load_ahead(act):
-        for k in THIRDS:
-            from_shard(first_owner(0, k, 0)[1], k, lambda src, k=k: pltpu.make_async_copy(
-                src, ahead.at[k], ahead_sem.at[k]), small=False, act=act)
 
     barrier = pltpu.get_barrier_semaphore()
     near = [flip(me, order[0]) for order in ORDERS]
     near += [flip(dev, 1) for dev in near] + [partner]
     for dev in near:
         pl.semaphore_signal(barrier, inc=1, device_id=(dev,), device_id_type=MESH)
-    load_ahead(lambda copy: copy.start())
     raw = [pltpu.make_async_copy(src, dst, raw_sem.at[i]) for i, (src, dst) in enumerate((
         (gg, wide_raw.at[0]), (gu, wide_raw.at[1]), (gq, q_raw), (gk, k_raw), (gv, v_raw), (gn, n_raw), (gqk, qk_raw)))]
     for copy in raw:
@@ -226,7 +223,6 @@
         start += tiles
     for f in PAIR:
         load_own(f, small=False)
-    load_ahead(lambda copy: copy.wait())
     pl.semaphore_wait(barrier, len(near))
     for f in THIRDS:
         send_first(f, small=False)
@@ -283,21 +279,26 @@
         copy.start()
 
     def r1_copy(slot, k, f):
-        return remote(emb.at[pl.ds(0, RS_TILES)], vout.at[slot_tiles(slot, k, f)], r1_send.at[slot, k, f],
+        return remote(emb.at[pl.ds(0, rs_tiles(k))], vout.at[slot_tiles(slot, k, f)], r1_send.at[slot, k, f],
                       r1_recv.at[slot, k, f], partner)
 
     def r2_copy(k, f):
-        return remote(s1.at[sum_rows(k, f)], r2.at[k, f], r2_send.at[k, f], r2_recv.at[k, f], flip(me, ORDERS[k][1]))
-
-    def r3_copy(k, half):
-        src = pl.ds(sum_rows(k, 2).start + half * HALF_ROWS, HALF_ROWS)
-        dst = pl.ds(half * HALF_ROWS, HALF_ROWS)
-        return remote(s1.at[src], r3.at[k, dst], r3_send.at[k, half], r3_recv.at[k, half], flip(me, ORDERS[k][2]))
+        return remote(s1.at[sum_rows(k, f)], r2.at[k, f, pl.ds(0, sum_rows(k, f).size)], r2_send.at[k, f], r2_recv.at[k, f], flip(me, ORDERS[k][1]))
+
+    def quarter(k, i):
+        return i * QUARTER, min((i + 1) * QUARTER, rs_tiles(k))
+
+    def r3_copy(k, i):
+        first, end = quarter(k, i)
+        rows = (end - first) * TILE_ROWS
+        src = pl.ds(sum_rows(k, 2).start + first * TILE_ROWS, rows)
+        dst = pl.ds(first * TILE_ROWS, rows)
+        return remote(s1.at[src], r3.at[k, dst], r3_send.at[k, i], r3_recv.at[k, i], flip(me, ORDERS[k][2]))
 
     for f in range(4):
         for k in THIRDS:
             pltpu.make_async_copy(
-                emb.at[pl.ds(0, RS_TILES)], vout.at[slot_tiles(3, k, f)], own_sem.at[k, f]).wait()
+                emb.at[pl.ds(0, rs_tiles(k))], vout.at[slot_tiles(3, k, f)], own_sem.at[k, f]).wait()
             for slot in (2, 0, 1):
                 r1_copy(slot, k, f).wait_recv()
 
@@ -309,7 +310,7 @@
                     s1[pl.ds(pl.multiple_of(row + 8 * j, 8), 8), :] = total[:, LANES * j:LANES * (j + 1)]
                 return 0
 
-            lax.fori_loop(0, RS_TILES, add_four, 0, unroll=2)
+            lax.fori_loop(0, rs_tiles(k), add_four, 0, unroll=2)
             if f < 2:
                 r2_copy(k, f).start()
     for f in PAIR:
@@ -322,10 +323,10 @@
                 s1[at, :] = s1[at, :] + r2[k, f, pl.ds(row, TILE_ROWS), :]
                 return 0
 
-            for half in PAIR:
-                lax.fori_loop(half * HALF_TILES, (half + 1) * HALF_TILES, add_two, 0, unroll=2)
+            for i in QUARTERS:
+                lax.fori_loop(*quarter(k, i), add_two, 0, unroll=2)
                 if f == 0:
-                    r3_copy(k, half).start()
+                    r3_copy(k, i).start()
 
     shift = LEAD - (SHARD_ROWS * me - TILE_ROWS * rs_start(me))
     for k in THIRDS:
@@ -346,15 +347,13 @@
 
     acc = jnp.zeros((TILE_ROWS, LANES), jnp.float32)
     end = (LEAD + SHARD_ROWS) // TILE_ROWS
-    for half in PAIR:
-        for k in THIRDS:
-            r3_copy(k, half).wait_recv()
-            lax.fori_loop(half * HALF_TILES, (half + 1) * HALF_TILES, functools.partial(finish, k), 0, unroll=2)
-        for k in THIRDS:
-            first = k * RS_TILES + 1
-            middle = first + HALF_TILES - 1
-            blocks = (middle, min(first + RS_TILES, end)) if half else (first, middle)
-            acc = lax.fori_loop(*blocks, squares, acc, unroll=3)
+    for i in QUARTERS:
+        for k in THIRDS:
+            r3_copy(k, i).wait_recv()
+            lax.fori_loop(*quarter(k, i), functools.partial(finish, k), 0, unroll=2)
+        for k in THIRDS:
+            blocks = [k * RS_TILES + q * QUARTER + (q % 4 == 0) for q in (i, i + 1)]
+            acc = lax.fori_loop(blocks[0], min(blocks[1], end), squares, acc, unroll=3)
     for copy in ext_copies:
         copy.start()
     nsend[...] = acc[0:8] + acc[8:16] + acc[16:24] + acc[24:32] + acc[32:40]
@@ -534,8 +533,8 @@
             for slot in THIRDS:
                 r1_copy(slot, k, f).wait_send()
     for k in THIRDS:
-        for half in PAIR:
-            r3_copy(k, half).wait_send()
+        for i in QUARTERS:
+            r3_copy(k, i).wait_send()
     for k in THIRDS:
         ag_arrived(k, 4)
         ag_across(k, 4)
@@ -637,7 +636,6 @@
                 pltpu.VMEM((3, PIECE_ROWS, LANES), f32),
                 pltpu.VMEM((3, TILE_ROWS, LANES), f32),
                 pltpu.SMEM((5,), f32),
-                pltpu.VMEM((3, RS_TILES, 8, WIDTH), bf16),
                 pltpu.VMEM((8, LANES), f32),
                 pltpu.VMEM((DEVS, 8, LANES), f32),
                 pltpu.VMEM((2, 3840, LANES), bf16),
@@ -648,12 +646,12 @@
                 pltpu.VMEM(shapes[9], bf16),
                 pltpu.VMEM((4, 8, WIDTH), bf16),
                 dma((7,)), dma((3,)), dma((3 + len(SMALL),)),
-                dma((3, 4)), dma((3, 3, 4)), dma((3, 3, 4)), dma((3, 2)), dma((3, 2)), dma((3, 2)), dma((3, 2)),
+                dma((3, 4)), dma((3, 3, 4)), dma((3, 3, 4)), dma((3, 2)), dma((3, 2)), dma((3, 4)), dma((3, 4)),
                 dma((4,)), dma((3,)), dma((3,)), dma((DEVS,)), dma((DEVS,)),
-                dma((3, 8)), dma((3, 8)), dma((3, 8)), dma((3, 8)), dma((3, LAST_PART + 1)), dma((3,)),
+                dma((3, 8)), dma((3, 8)), dma((3, 8)), dma((3, 8)), dma((3, LAST_PART + 1)),
             ],
             compiler_params=pltpu.CompilerParams(
-                collective_id=0, has_side_effects=True, vmem_limit_bytes=26_960_000),
+                collective_id=0, has_side_effects=True, vmem_limit_bytes=26_500_000),
         )(*tiled, *state, arrays[GRAD_COUNT + 3])
         kept = [pltpu.with_memory_space_constraint(arr, pltpu.VMEM) for arr in kept]
         outs = pl.pallas_call(

time: 271 us -> 268 us (0.989)
  Pallas kernels: 270 us -> 267 us
    pallas_call x1, Pallas kernels: 259 us -> 256 us  [local_update(): pl.pallas_call(kernel, out_shape=[pltpu.VMEM((SHARD_ROWS, LANES), f32)] *...]
where the time goes in v7:
time: 268 us
  Pallas kernels  267 us (100%)
    pallas_call x1, Pallas kernels, local_update(): pl.pallas_call(kernel, out_shape=[pltpu.VMEM((SHARD_ROWS, LANES), f32)] *...  256 us
    pallas_call x1, Pallas kernels, local_update(): pl.pallas_call(flush, out_shape=[jax.ShapeDtypeStruct((EMBED_TILES, 8, WI...  11.4 us

profile of v7, /device:TPU:0, one launch (start us, length us, event | category | flops | bytes accessed | tf_op | source)
XLA Modules:
  0.0 267.8 jit_solution(2489994138862995177)
XLA Ops:
  0.7 255.8 %shard_map.237 = (f32[6149,128]{1,0:T(8,128)S(1)}, f32[6149,128]{1,0:T(8,128)S(1)}, f32[6149,128]{1,0:T(8,128)S(1)}, bf16[2496,8,640]{2,1,0:T(8,128)(2,1)S(1)}, bf16[463,8,640]{2,1,0:T(8,128)(2,1)}) custom-call(bf16[2048,8,640]{2,1,0:T(8,128)(2,1)} %bitcast.42, bf16[48,8,640]{2,1,0:T(8,128)(2,1)} %bitcast.49, bf16[12,8,640]{2,1,0:T(8,128)(2,1)} %bitcast.51, ...), custom_call_target="tpu_custom_call" | custom-call | tf_op jit(solution)/shard_map/pallas_call | solution.py:626
  256.4 11.4 %shard_map.238 = (bf16[2048,8,640]{2,1,0:T(8,128)(2,1)}, bf16[48,8,640]{2,1,0:T(8,128)(2,1)}, bf16[12,8,640]{2,1,0:T(8,128)(2,1)}, bf16[12,8,640]{2,1,0:T(8,128)...) custom-call(f32[6149,128]{1,0:T(8,128)S(1)} %get-tuple-element.30.mo, ...), custom_call_target="tpu_custom_call" | custom-call | tf_op jit(solution)/shard_map/pallas_call | solution.py:657

commit v8 on v7

--- a/solution.py
+++ b/solution.py
@@ -354,21 +354,22 @@
         for k in THIRDS:
             blocks = [k * RS_TILES + q * QUARTER + (q % 4 == 0) for q in (i, i + 1)]
             acc = lax.fori_loop(blocks[0], min(blocks[1], end), squares, acc, unroll=3)
+    start = end * TILE_ROWS
+    total = jnp.sum(acc, axis=0, keepdims=True)
+    for row, rows in ((start, 24), (start + 24, 5)):
+        part = grad[pl.ds(row, rows), :]
+        total = total + jnp.sum(part * part, axis=0, keepdims=True)
+    nsend[...] = total
+
+    others = [flip_mask(me, (1, 2, 4, 8), mask) for mask in sorted(OTHERS, key=lambda mask: -(mask // 2).bit_count())]
+
+    def n_copy(i, source):
+        return remote(nsend, nrecv.at[source], n_send.at[i], n_recv.at[source], others[i])
+
+    for i in range(len(others)):
+        n_copy(i, me).start()
     for copy in ext_copies:
         copy.start()
-    nsend[...] = acc[0:8] + acc[8:16] + acc[16:24] + acc[24:32] + acc[32:40]
-    start = end * TILE_ROWS
-    for row, rows in ((start, 8), (start + 8, 8), (start + 16, 8), (start + 24, 5)):
-        part = grad[pl.ds(row, rows), :]
-        nsend[0:rows, :] = nsend[0:rows, :] + part * part
-
-    others = [flip_mask(me, (1, 2, 4, 8), mask) for mask in sorted(OTHERS, key=lambda mask: -(mask // 2).bit_count())]
-
-    def n_copy(i, source):
-        return remote(nsend, nrecv.at[source], n_send.at[i], n_recv.at[source], others[i])
-
-    for i in range(len(others)):
-        n_copy(i, me).start()
 
     for copy in state:
         copy.wait()
@@ -380,17 +381,12 @@
     rest_one, rest_two = 1.0 - beta_one, 1.0 - beta_two
     hat_one = 1.0 / (1.0 - lax.integer_pow(beta_one, ADAM_STEP))
     hat_two = 1.0 / (1.0 - lax.integer_pow(beta_two, ADAM_STEP))
-    for copy in ext_copies:
-        copy.wait_recv()
 
     for i, dev in enumerate(others):
         n_copy(i, me).wait_send()
         n_copy(i, dev).wait_recv()
     nrecv[me] = nsend[...]
-    total = nrecv[0]
-    for j in OTHERS:
-        total = total + nrecv[j]
-    total = jnp.sum(jnp.sum(total, axis=1, keepdims=True), axis=0, keepdims=True)
+    total = jnp.sum(jnp.sum(nrecv[...], axis=0), axis=1, keepdims=True)
     clip = jnp.minimum(1.0, max_norm / (jnp.sqrt(jnp.broadcast_to(total, (8, LANES))) + CLIP_EPS))
 
     def wide(value, rows):
@@ -484,6 +480,8 @@
         if k == 2:
             adam_rows(6120, 24)
             adam_rows(6144, 5)
+            for copy in ext_copies:
+                copy.wait_recv()
             at = pl.ds(LEAD + SHARD_ROWS, TILE_ROWS)
             _, _, p = adam(grad[at, :], ext[0], ext[1], ext[2], SHARD_ROWS * (me + 1), TILE_ROWS)
             grad[at, :] = p
@@ -507,9 +505,9 @@
         else:
             send(count)
 
-    own_part(0, 0, 7, (0, 8))
-    own_part(0, 7, 14, (8, 22))
-    own_part(0, 21, 30, (22, 52))
+    own_part(0, 0, 4, (0, 5))
+    own_part(0, 4, 12, (5, 17))
+    own_part(0, 16, 35, (17, 52))
     own_part(1, 0, AG_TILES, (52, 103))
     own_part(2, 0, None, (103, 153))
     for k in THIRDS:
@@ -636,8 +634,8 @@
                 pltpu.VMEM((3, PIECE_ROWS, LANES), f32),
                 pltpu.VMEM((3, TILE_ROWS, LANES), f32),
                 pltpu.SMEM((5,), f32),
-                pltpu.VMEM((8, LANES), f32),
-                pltpu.VMEM((DEVS, 8, LANES), f32),
+                pltpu.VMEM((1, LANES), f32),
+                pltpu.VMEM((DEVS, 1, LANES), f32),
                 pltpu.VMEM((2, 3840, LANES), bf16),
                 pltpu.VMEM((48, 8, WIDTH), bf16),
                 pltpu.VMEM((12, 8, WIDTH), bf16),

time: 268 us -> 267 us (level)
  no operation moved by 1% of the time
where the time goes in v8:
time: 267 us; the launch traced here: 266 us
  Pallas kernels  266 us (100%)
    pallas_call x1, Pallas kernels, local_update(): pl.pallas_call(kernel, out_shape=[pltpu.VMEM((SHARD_ROWS, LANES), f32)] *...  254 us
    pallas_call x1, Pallas kernels, local_update(): pl.pallas_call(flush, out_shape=[jax.ShapeDtypeStruct((EMBED_TILES, 8, WI...  11.4 us

profile of v8, /device:TPU:0, one launch (start us, length us, event | category | flops | bytes accessed | tf_op | source)
XLA Modules:
  0.0 266.5 jit_solution(300037980774059881)
XLA Ops:
  0.7 254.5 %shard_map.237 = (f32[6149,128]{1,0:T(8,128)S(1)}, f32[6149,128]{1,0:T(8,128)S(1)}, f32[6149,128]{1,0:T(8,128)S(1)}, bf16[2496,8,640]{2,1,0:T(8,128)(2,1)S(1)}, bf16[463,8,640]{2,1,0:T(8,128)(2,1)}) custom-call(bf16[2048,8,640]{2,1,0:T(8,128)(2,1)} %bitcast.42, bf16[48,8,640]{2,1,0:T(8,128)(2,1)} %bitcast.49, bf16[12,8,640]{2,1,0:T(8,128)(2,1)} %bitcast.51, ...), custom_call_target="tpu_custom_call" | custom-call | tf_op jit(solution)/shard_map/pallas_call | solution.py:624
  255.1 11.4 %shard_map.238 = (bf16[2048,8,640]{2,1,0:T(8,128)(2,1)}, bf16[48,8,640]{2,1,0:T(8,128)(2,1)}, bf16[12,8,640]{2,1,0:T(8,128)(2,1)}, bf16[12,8,640]{2,1,0:T(8,128)...) custom-call(f32[6149,128]{1,0:T(8,128)S(1)} %get-tuple-element.30.mo, ...), custom_call_target="tpu_custom_call" | custom-call | tf_op jit(solution)/shard_map/pallas_call | solution.py:655

commit v9 on v8

--- a/solution.py
+++ b/solution.py
@@ -71,7 +71,7 @@
 SPARE = 42 * RS_TILES
 PIECE_ROWS = RS_TILES * TILE_ROWS
 QUARTERS = range(4)
-QUARTER = RS_TILES // 4
+QUARTER = 16
 
 
 def slot_tiles(slot, k, f):
@@ -352,7 +352,7 @@
             r3_copy(k, i).wait_recv()
             lax.fori_loop(*quarter(k, i), functools.partial(finish, k), 0, unroll=2)
         for k in THIRDS:
-            blocks = [k * RS_TILES + q * QUARTER + (q % 4 == 0) for q in (i, i + 1)]
+            blocks = [k * RS_TILES + min(q * QUARTER, RS_TILES) + (q % 4 == 0) for q in (i, i + 1)]
             acc = lax.fori_loop(blocks[0], min(blocks[1], end), squares, acc, unroll=3)
     start = end * TILE_ROWS
     total = jnp.sum(acc, axis=0, keepdims=True)
@@ -476,7 +476,7 @@
     base = LEAD + TILE_ROWS * ag_start(me) - SHARD_ROWS * me
 
     def own_part(k, skip, count, blocks):
-        lax.fori_loop(*blocks, adam_block, 0)
+        lax.fori_loop(*blocks, adam_block, 0, unroll=2)
         if k == 2:
             adam_rows(6120, 24)
             adam_rows(6144, 5)

time: 267 us -> 266 us (level)
  no operation moved by 1% of the time
where the time goes in v9:
time: 266 us
  Pallas kernels  266 us (100%)
    pallas_call x1, Pallas kernels, local_update(): pl.pallas_call(kernel, out_shape=[pltpu.VMEM((SHARD_ROWS, LANES), f32)] *...  254 us
    pallas_call x1, Pallas kernels, local_update(): pl.pallas_call(flush, out_shape=[jax.ShapeDtypeStruct((EMBED_TILES, 8, WI...  11.4 us

profile of v9, /device:TPU:0, one launch (start us, length us, event | category | flops | bytes accessed | tf_op | source)
XLA Modules:
  0.0 266.2 jit_solution(628020408371414554)
XLA Ops:
  0.7 254.2 %shard_map.237 = (f32[6149,128]{1,0:T(8,128)S(1)}, f32[6149,128]{1,0:T(8,128)S(1)}, f32[6149,128]{1,0:T(8,128)S(1)}, bf16[2496,8,640]{2,1,0:T(8,128)(2,1)S(1)}, bf16[463,8,640]{2,1,0:T(8,128)(2,1)}) custom-call(bf16[2048,8,640]{2,1,0:T(8,128)(2,1)} %bitcast.42, bf16[48,8,640]{2,1,0:T(8,128)(2,1)} %bitcast.49, bf16[12,8,640]{2,1,0:T(8,128)(2,1)} %bitcast.51, ...), custom_call_target="tpu_custom_call" | custom-call | tf_op jit(solution)/shard_map/pallas_call | solution.py:624
  254.9 11.4 %shard_map.238 = (bf16[2048,8,640]{2,1,0:T(8,128)(2,1)}, bf16[48,8,640]{2,1,0:T(8,128)(2,1)}, bf16[12,8,640]{2,1,0:T(8,128)(2,1)}, bf16[12,8,640]{2,1,0:T(8,128)...) custom-call(f32[6149,128]{1,0:T(8,128)S(1)} %get-tuple-element.30.mo, ...), custom_call_target="tpu_custom_call" | custom-call | tf_op jit(solution)/shard_map/pallas_call | solution.py:655

commit v10 on v9

--- a/solution.py
+++ b/solution.py
@@ -29,7 +29,7 @@
 RS_TILES = 52
 TAIL_TILES = (SHARD_ROWS * 15) // TILE_ROWS + 3 * RS_TILES - TAIL_START
 AG_TILES = 51
-PART_TILES = 16
+PART_STARTS = (0, 24, 40, 48)
 LAST_PART = 3
 FLUSH_PARTS = 4
 LEAD = 40
@@ -448,11 +448,11 @@
 
     def ag_part(k, mask, i, run):
         owner = flip_mask(me, ORDERS[k], mask)
-        first = ag_start(owner) + k * AG_TILES + i * PART_TILES
+        first = ag_start(owner) + k * AG_TILES + PART_STARTS[i]
         if i < LAST_PART:
-            run(vout.at[pl.ds(first, PART_TILES)])
+            run(vout.at[pl.ds(first, PART_STARTS[i + 1] - PART_STARTS[i])])
         else:
-            ag_sizes(owner, k, lambda size: run(vout.at[pl.ds(first, size - LAST_PART * PART_TILES)]))
+            ag_sizes(owner, k, lambda size: run(vout.at[pl.ds(first, size - PART_STARTS[i])]))
 
     def last_copy(k, i, part):
         return remote(part, part, ag_send.at[k, 7], last_recv.at[k, i], flip(me, ORDERS[k][2]))

time: 266 us -> 266 us (level)
  no operation moved by 1% of the time
where the time goes in v10:
time: 266 us
  Pallas kernels  265 us (100%)
    pallas_call x1, Pallas kernels, local_update(): pl.pallas_call(kernel, out_shape=[pltpu.VMEM((SHARD_ROWS, LANES), f32)] *...  254 us
    pallas_call x1, Pallas kernels, local_update(): pl.pallas_call(flush, out_shape=[jax.ShapeDtypeStruct((EMBED_TILES, 8, WI...  11.4 us

profile of v10, /device:TPU:0, one launch (start us, length us, event | category | flops | bytes accessed | tf_op | source)
XLA Modules:
  0.0 266.1 jit_solution(14545153967410672728)
XLA Ops:
  0.7 254.1 %shard_map.237 = (f32[6149,128]{1,0:T(8,128)S(1)}, f32[6149,128]{1,0:T(8,128)S(1)}, f32[6149,128]{1,0:T(8,128)S(1)}, bf16[2496,8,640]{2,1,0:T(8,128)(2,1)S(1)}, bf16[463,8,640]{2,1,0:T(8,128)(2,1)}) custom-call(bf16[2048,8,640]{2,1,0:T(8,128)(2,1)} %bitcast.42, bf16[48,8,640]{2,1,0:T(8,128)(2,1)} %bitcast.49, bf16[12,8,640]{2,1,0:T(8,128)(2,1)} %bitcast.51, ...), custom_call_target="tpu_custom_call" | custom-call | tf_op jit(solution)/shard_map/pallas_call | solution.py:624
  254.7 11.4 %shard_map.238 = (bf16[2048,8,640]{2,1,0:T(8,128)(2,1)}, bf16[48,8,640]{2,1,0:T(8,128)(2,1)}, bf16[12,8,640]{2,1,0:T(8,128)(2,1)}, bf16[12,8,640]{2,1,0:T(8,128)...) custom-call(f32[6149,128]{1,0:T(8,128)S(1)} %get-tuple-element.30.mo, ...), custom_call_target="tpu_custom_call" | custom-call | tf_op jit(solution)/shard_map/pallas_call | solution.py:655
